TPU v7x, 64 devices: a 2x2x8 block of a 4x4x8 slice. The times are simulated.
64 devices in a mesh: dp: 4 (over x, y), tp: 16 (over z, core).
Axes of the slice: x: 2, y: 2, z: 8, core: 2. Of those that a mesh axis runs over, the one named last changes fastest.
The devices are a block of a 4x4x8 slice.
Arguments:
- x_in: bfloat16 [4, 4096, 1024], P('dp', 'tp'), parts along dimension 0
- x_mid: bfloat16 [4, 4096, 1024], P('dp', 'tp'), parts along dimension 0
- d_out: bfloat16 [4, 4096, 1024], P('dp', 'tp'), parts along dimension 0
- q_saved: bfloat16 [4, 4096, 16, 64], P('dp', None, 'tp'), parts along dimension 0
- k_saved: bfloat16 [4, 4096, 16, 64], P('dp', None, 'tp'), parts along dimension 0
- v_saved: bfloat16 [4, 4096, 16, 64], P('dp', None, 'tp'), parts along dimension 0
- z_saved: bfloat16 [4, 4096, 4096], P('dp', None, 'tp'), parts along dimension 0
- ln1_gain: float32 [1024], replicated
- ln1_bias: float32 [1024], replicated
- ln2_gain: float32 [1024], replicated
- ln2_bias: float32 [1024], replicated
- w_qkv: bfloat16 [3, 1024, 16, 64], P(None, None, 'tp')
- w_proj: bfloat16 [16, 64, 1024], P('tp')
- w_fc1: bfloat16 [1024, 4096], P(None, 'tp')
- w_fc2: bfloat16 [4096, 1024], P('tp')
Outputs:
- output 1: bfloat16 [4, 4096, 1024], P('dp', 'tp'), parts along dimension 0
- output 2: float32 [12, 1024, 16, 64], P('dp', None, 'tp'), parts along dimension 0
- output 3: float32 [12, 16, 64], P('dp', 'tp'), parts along dimension 0
- output 4: float32 [64, 64, 1024], P(('dp', 'tp')), parts along dimension 0
- output 5: float32 [4096, 4096], P('dp', 'tp'), parts along dimension 0
- output 6: float32 [16384], P(('dp', 'tp')), parts along dimension 0
- output 7: float32 [16384, 1024], P(('dp', 'tp')), parts along dimension 0
- output 8: float32 [24, 1024], P('dp'), parts along dimension 0
There are 4 independent parts. A program takes and returns all parts, laid end to end along the dimension named above; an argument that names none is the same for every part.
All inputs are finite; a program needn't handle non-finite values.
Results may differ from a plain program's by a relative error of at most 0.0129028.
Values are sent between devices in bfloat16 or wider.
A program may use at most 768 MiB of HBM per device.

v0:
```python
import jax
import jax.numpy as jnp
from jax import lax
from jax.sharding import PartitionSpec as P

LN_EPS = 1e-5
GELU_COEF = 0.044715
GELU_SCALE = 0.7978845608028654


def layer_norm_fwd(token_rows, norm_gain, norm_bias):
    rows_f32 = token_rows.astype(jnp.float32)
    centered = rows_f32 - jnp.mean(rows_f32, axis=-1, keepdims=True)
    inv_std = lax.rsqrt(jnp.mean(centered * centered, axis=-1, keepdims=True) + LN_EPS)
    x_hat = centered * inv_std
    return x_hat, inv_std, (x_hat * norm_gain + norm_bias).astype(jnp.bfloat16)


def layer_norm_bwd(grad_norm, x_hat, inv_std, norm_gain):
    grad_hat = grad_norm * norm_gain
    centered_grad = grad_hat - jnp.mean(grad_hat, axis=-1, keepdims=True)
    return inv_std * (centered_grad - x_hat * jnp.mean(grad_hat * x_hat, axis=-1, keepdims=True))


def gelu_parts(pre_act):
    tanh_val = jnp.tanh(GELU_SCALE * (pre_act + GELU_COEF * pre_act * pre_act * pre_act))
    act_value = 0.5 * pre_act * (1.0 + tanh_val)
    act_slope = 0.5 * (1.0 + tanh_val) + 0.5 * pre_act * (1.0 - tanh_val * tanh_val) * GELU_SCALE * (1.0 + 3.0 * GELU_COEF * pre_act * pre_act)
    return act_value, act_slope


def attention_grads(q_heads, k_heads, v_heads, grad_ctx):
    seq_len = q_heads.shape[1]
    score_scale = q_heads.shape[-1] ** -0.5
    scores = jnp.einsum('bqhe,bkhe->bhqk', q_heads, k_heads, preferred_element_type=jnp.float32) * score_scale
    row_ids = lax.broadcasted_iota(jnp.int32, (seq_len, seq_len), 0)
    col_ids = lax.broadcasted_iota(jnp.int32, (seq_len, seq_len), 1)
    scores = jnp.where(row_ids >= col_ids, scores, -1e30)
    attn_probs = jax.nn.softmax(scores, axis=-1)
    probs_low = attn_probs.astype(jnp.bfloat16)
    context = jnp.einsum('bhqk,bkhe->bqhe', probs_low, v_heads, preferred_element_type=jnp.float32).astype(jnp.bfloat16)
    grad_probs = jnp.einsum('bqhe,bkhe->bhqk', grad_ctx, v_heads, preferred_element_type=jnp.float32)
    grad_scores = (attn_probs * (grad_probs - jnp.sum(grad_probs * attn_probs, axis=-1, keepdims=True)) * score_scale).astype(jnp.bfloat16)
    grad_q = jnp.einsum('bhqk,bkhe->bqhe', grad_scores, k_heads, preferred_element_type=jnp.float32).astype(jnp.bfloat16)
    grad_k = jnp.einsum('bhqk,bqhe->bkhe', grad_scores, q_heads, preferred_element_type=jnp.float32).astype(jnp.bfloat16)
    grad_v = jnp.einsum('bhqk,bqhe->bkhe', probs_low, grad_ctx, preferred_element_type=jnp.float32).astype(jnp.bfloat16)
    return context, grad_q, grad_k, grad_v


def solution(mesh):
    def local_backward(x_in, x_mid, d_out, q_saved, k_saved, v_saved, z_saved, ln1_gain, ln1_bias, ln2_gain, ln2_bias, w_qkv, w_proj, w_fc1, w_fc2):
        norm2_hat, norm2_rstd, h2_local = layer_norm_fwd(x_mid, ln2_gain, ln2_bias)
        h2_full = lax.all_gather(h2_local, 'tp', axis=1, tiled=True)
        dout_full = lax.all_gather(d_out, 'tp', axis=1, tiled=True)
        act_value, act_slope = gelu_parts(z_saved.astype(jnp.float32))
        grad_wfc2 = jnp.einsum('bsf,bsd->fd', act_value.astype(jnp.bfloat16), dout_full, preferred_element_type=jnp.float32)
        grad_pre = (jnp.einsum('bsd,fd->bsf', dout_full, w_fc2, preferred_element_type=jnp.float32) * act_slope).astype(jnp.bfloat16)
        grad_wfc1 = jnp.einsum('bsd,bsf->df', h2_full, grad_pre, preferred_element_type=jnp.float32)
        grad_bfc1 = jnp.sum(grad_pre, axis=(0, 1), dtype=jnp.float32)
        h2_partial = jnp.einsum('bsf,df->bsd', grad_pre, w_fc1, preferred_element_type=jnp.float32).astype(jnp.bfloat16)
        grad_h2 = lax.psum_scatter(h2_partial, 'tp', scatter_dimension=1, tiled=True).astype(jnp.float32)
        grad_mid = (d_out.astype(jnp.float32) + layer_norm_bwd(grad_h2, norm2_hat, norm2_rstd, ln2_gain)).astype(jnp.bfloat16)
        mid_full = lax.all_gather(grad_mid, 'tp', axis=1, tiled=True)
        norm1_hat, norm1_rstd, h1_local = layer_norm_fwd(x_in, ln1_gain, ln1_bias)
        h1_full = lax.all_gather(h1_local, 'tp', axis=1, tiled=True)
        grad_ctx = jnp.einsum('bsd,hed->bshe', mid_full, w_proj, preferred_element_type=jnp.float32).astype(jnp.bfloat16)
        context, grad_q, grad_k, grad_v = attention_grads(q_saved, k_saved, v_saved, grad_ctx)
        grad_wproj = jnp.einsum('bshe,bsd->hed', context, mid_full, preferred_element_type=jnp.float32)
        qkv_grads = jnp.stack([grad_q, grad_k, grad_v])
        grad_wqkv = jnp.einsum('bsd,ibshe->idhe', h1_full, qkv_grads, preferred_element_type=jnp.float32)
        grad_bqkv = jnp.sum(qkv_grads, axis=(1, 2), dtype=jnp.float32)
        h1_partial = jnp.einsum('ibshe,idhe->bsd', qkv_grads, w_qkv, preferred_element_type=jnp.float32).astype(jnp.bfloat16)
        grad_h1 = lax.psum_scatter(h1_partial, 'tp', scatter_dimension=1, tiled=True).astype(jnp.float32)
        grad_x = (grad_mid.astype(jnp.float32) + layer_norm_bwd(grad_h1, norm1_hat, norm1_rstd, ln1_gain)).astype(jnp.bfloat16)
        vec_partial = jnp.stack([
            jnp.sum(grad_h1 * norm1_hat, axis=(0, 1)),
            jnp.sum(grad_h1, axis=(0, 1)),
            jnp.sum(grad_h2 * norm2_hat, axis=(0, 1)),
            jnp.sum(grad_h2, axis=(0, 1)),
            jnp.sum(grad_mid, axis=(0, 1), dtype=jnp.float32),
            jnp.sum(d_out, axis=(0, 1), dtype=jnp.float32),
        ])
        grad_vecs = lax.psum(vec_partial, 'tp')
        return grad_x, grad_wqkv, grad_bqkv, grad_wproj, grad_wfc1, grad_bfc1, grad_wfc2, grad_vecs

    tok_spec = P('dp', 'tp', None)
    head_spec = P('dp', None, 'tp', None)
    in_specs = (tok_spec, tok_spec, tok_spec, head_spec, head_spec, head_spec, P('dp', None, 'tp'),
                P(None), P(None), P(None), P(None),
                P(None, None, 'tp', None), P('tp', None, None), P(None, 'tp'), P('tp', None))
    out_specs = (tok_spec, P('dp', None, 'tp', None), P('dp', 'tp', None), P(('dp', 'tp'), None, None),
                 P('dp', 'tp'), P(('dp', 'tp')), P(('dp', 'tp'), None), P('dp', None))
    return jax.shard_map(local_backward, mesh=mesh, in_specs=in_specs, out_specs=out_specs, check_vma=False)
```

profile of v0, /device:TPU:21, one launch (start us, length us, event | category | flops | bytes accessed | tf_op | source)
XLA Modules:
  0.0 597.9 jit_solution(11627576795077385855)
XLA Ops:
  8.1 59.1 %all-gather.5.cloned.1.call-done = bf16[1,4096,1024]{2,1,0:T(8,128)(2,1)} async-done(((bf16[1,256,1024]{2,1,0:T(8,128)(2,1)}), bf16[1,4096,1024]{2,1,0:T(8,128)(2,1)}) %all-gather.5.cloned.1.call-update) | async-done | bytes 8388624 | tf_op jit(solution)/shard_map/all_gather | solution.py:54
  67.2 9.4 %convert_reduce_fusion = (f32[256]{0:T(256)}, bf16[1,4096,256]{2,1,0:T(8,128)(2,1)S(1)}) fusion(bf16[1,4096,256]{2,1,0:T(8,128)(2,1)} %param.21, bf16[256,1024]{1,0:T(8,128)(2,1)} %param.29, bf16[1,4096,1024]{2,1,0:T(8,128)(2,1)} %all-gather.5.cloned.1.call-done), kind=kOutput, calls=%fused_computation.54 | convolution fusion | flops 2170552064 | bytes 13108224 | tf_op jit(solution)/shard_map/bsd,fd->bsf/dot_general | solution.py:57
  77.9 5.6 convert_bitcast_fusion
  84.1 62.5 %reduce-scatter.3.cloned.1.call-done = bf16[1,256,1024]{2,1,0:T(8,128)(2,1)} async-done(((bf16[1,4096,1024]{2,1,0:T(8,128)(2,1)}), bf16[1,256,1024]{2,1,0:T(8,128)(2,1)}) %reduce-scatter.3.cloned.1.call-update) | async-done | bytes 524304 | tf_op jit(solution)/shard_map/reduce_scatter | solution.py:61
  146.5 3.0 fusion.102
  149.5 3.0 convert_reduce_fusion.5
  153.1 23.8 %fusion.2 = (f32[4096]{0:T(1024)S(1)}, f32[4096,4096]{0,1:T(8,128)}) fusion(bf16[1,4096,1,64]{1,3,2,0:T(8,128)(2,1)S(1)} %copy-done.14, bf16[1,4096,1,64]{1,3,2,0:T(8,128)(2,1)S(1)} %copy-done), kind=kOutput, calls=%fused_computation.7 | convolution fusion | flops 2214588416 | bytes 68173824 | tf_op jit(solution)/shard_map/bqhe,bkhe->bhqk/dot_general | solution.py:35
  177.0 21.8 %fusion.1 = f32[4096]{0:T(1024)S(1)} fusion(f32[4096,4096]{0,1:T(8,128)} %get-tuple-element.30, f32[4096]{0:T(1024)S(1)} %get-tuple-element.29), kind=kLoop, calls=%fused_computation.6 | loop fusion | flops 83881984 | bytes 67141632 | tf_op jit(solution)/shard_map/reduce_sum | solution.py:39
  198.7 8.6 %all-gather.7.cloned.1.call-done = bf16[1,4096,1024]{2,1,0:T(8,128)(2,1)} async-done(((bf16[1,256,1024]{2,1,0:T(8,128)(2,1)}), bf16[1,4096,1024]{2,1,0:T(8,128)(2,1)}) %all-gather.7.cloned.1.call-update) | async-done | bytes 8388624 | tf_op jit(solution)/shard_map/all_gather | solution.py:63
  207.3 6.0 %fusion.31 = bf16[4096,64]{0,1:T(8,128)(2,1)S(1)} fusion(bf16[1,4096,1024]{2,1,0:T(8,128)(2,1)} %all-gather.7.cloned.1.call-done, bf16[1,64,1024]{2,1,0:T(8,128)(2,1)S(1)} %copy-done.19), kind=kOutput, calls=%fused_computation.40 | convolution fusion | flops 537133056 | bytes 9043968 | tf_op jit(solution)/shard_map/bsd,hed->bshe/dot_general | solution.py:66
  213.4 28.9 %fusion.41 = bf16[1,1,4096,1,64]{2,4,3,1,0:T(8,128)(2,1)} fusion(bf16[4096,64]{0,1:T(8,128)(2,1)S(1)} %fusion.31, f32[4096,4096]{0,1:T(8,128)} %get-tuple-element.30, f32[4096]{0:T(1024)S(1)} %fusion.1, f32[4096]{0:T(1024)S(1)} %get-tuple-element.29), kind=kOutput, calls=%fused_computation.45 | convolution fusion | flops 2248409088 | bytes 68190208 | tf_op jit(solution)/shard_map/bhqk,bqhe->bkhe/dot_general | solution.py:46
  242.2 48.6 %multiply_reduce_fusion = (f32[4096]{0:T(1024)S(1)}, f32[4096,4096]{0,1:T(8,128)}) fusion(f32[4096]{0:T(1024)S(1)} %fusion.1, f32[4096]{0:T(1024)S(1)} %get-tuple-element.29, f32[4096,4096]{0,1:T(8,128)} %get-tuple-element.30, bf16[4096,64]{0,1:T(8,128)(2,1)S(1)} %fusion.31, bf16[1,4096,1,64]{1,3,2,0:T(8,128)(2,1)S(1)} %copy-done.28), kind=kOutput, calls=%fused_computation.1 | convolution fusion | flops 2264920064 | bytes 135315456 | tf_op jit(solution)/shard_map/bqhe,bkhe->bhqk/dot_general | solution.py:42
  290.9 53.4 %multiply_convert_fusion = bf16[4096,4096]{0,1:T(8,128)(2,1)} fusion(f32[4096,4096]{0,1:T(8,128)} %get-tuple-element.32, f32[4096]{0:T(1024)S(1)} %get-tuple-element.31, f32[4096]{0:T(1024)S(1)} %fusion.1, f32[4096]{0:T(1024)S(1)} %get-tuple-element.29, f32[4096,4096]{0,1:T(8,128)} %get-tuple-element.30), kind=kLoop, calls=%fused_computation | loop fusion | flops 150994944 | bytes 167821312 | tf_op jit(solution)/shard_map/convert_element_type | solution.py:43
  344.3 16.2 %fusion.44 = bf16[1,1,4096,1,64]{2,4,3,1,0:T(8,128)(2,1)S(1)} fusion(bf16[4096,4096]{0,1:T(8,128)(2,1)} %multiply_convert_fusion, bf16[1,4096,1,64]{1,3,2,0:T(8,128)(2,1)S(1)} %copy-done), kind=kOutput, calls=%fused_computation.46 | convolution fusion | flops 2147745792 | bytes 34603008 | tf_op jit(solution)/shard_map/bhqk,bqhe->bkhe/dot_general | solution.py:45
  360.6 14.0 %fusion.40 = bf16[1,1,4096,1,64]{2,4,3,1,0:T(8,128)(2,1)S(1)} fusion(bf16[4096,4096]{0,1:T(8,128)(2,1)} %multiply_convert_fusion, bf16[1,4096,1,64]{1,3,2,0:T(8,128)(2,1)S(1)} %copy-done.15), kind=kOutput, calls=%fused_computation.44 | convolution fusion | flops 2147745792 | bytes 34603008 | tf_op jit(solution)/shard_map/bhqk,bkhe->bqhe/dot_general | solution.py:44
  375.5 5.6 fusion.19
  382.6 61.4 %reduce-scatter.5.cloned.1.call-done = bf16[1,256,1024]{2,1,0:T(8,128)(2,1)} async-done(((bf16[1,4096,1024]{2,1,0:T(8,128)(2,1)}), bf16[1,256,1024]{2,1,0:T(8,128)(2,1)}) %reduce-scatter.5.cloned.1.call-update) | async-done | bytes 524304 | tf_op jit(solution)/shard_map/reduce_scatter | solution.py:73
  444.0 2.4 fusion.103
  446.5 7.7 %fusion.15 = f32[256,1024]{1,0:T(8,128)} fusion(bf16[1,4096,1024]{2,1,0:T(8,128)(2,1)} %all-gather.5.cloned.1.call-done, bf16[1,4096,256]{2,1,0:T(8,128)(2,1)} %param.21), kind=kOutput, calls=%fused_computation.28 | convolution fusion | flops 2157969408 | bytes 11534336 | tf_op jit(solution)/shard_map/bsf,bsd->fd/dot_general | solution.py:56
  455.1 45.7 %all-gather.11.cloned.1.call-done = bf16[1,4096,1024]{2,1,0:T(8,128)(2,1)} async-done(((bf16[1,256,1024]{2,1,0:T(8,128)(2,1)}), bf16[1,4096,1024]{2,1,0:T(8,128)(2,1)}) %all-gather.11.cloned.1.call-update) | async-done | bytes 8388624 | tf_op jit(solution)/shard_map/all_gather | solution.py:53
  500.8 6.7 %fusion.7 = f32[1024,256]{1,0:T(8,128)} fusion(bf16[1,4096,1024]{2,1,0:T(8,128)(2,1)} %all-gather.11.cloned.1.call-done, bf16[1,4096,256]{2,1,0:T(8,128)(2,1)S(1)} %copy-done.2), kind=kOutput, calls=%fused_computation.20 | convolution fusion | flops 2147483648 | bytes 11534336 | tf_op jit(solution)/shard_map/bsd,bsf->df/dot_general | solution.py:58
  507.6 30.8 %fusion.83 = f32[1,64,1024]{2,1,0:T(8,128)} fusion(bf16[1,4096,1024]{2,1,0:T(8,128)(2,1)} %all-gather.7.cloned.1.call-done, bf16[1,4096,1,64]{1,3,2,0:T(8,128)(2,1)} %param.20, f32[4096,4096]{0,1:T(8,128)} %get-tuple-element.30, f32[4096]{0:T(1024)S(1)} %fusion.1, f32[4096]{0:T(1024)S(1)} %get-tuple-element.29), kind=kOutput, calls=%fused_computation.95 | convolution fusion | flops 2785280000 | bytes 76316672 | tf_op jit(solution)/shard_map/bshe,bsd->hed/dot_general | solution.py:68
  538.4 44.6 %psum.7 = f32[6,1024]{1,0:T(8,128)} all-reduce(f32[6,1024]{1,0:T(8,128)S(1)} %stack.43), channel_id=1, replica_groups=mesh['dp'=4,'tp'=16] {'tp'}, use_global_device_ids=true, to_apply=%region_21.22 | all-reduce | flops 6144 | bytes 49152 | tf_op jit(solution)/shard_map/psum | solution.py:83
  584.3 6.2 %fusion.70 = f32[3,1024,1,64]{1,3,2,0:T(8,128)} fusion(bf16[1,4096,1024]{2,1,0:T(8,128)(2,1)} %all-gather.9.cloned.1.call-done, bf16[1,1,4096,1,64]{2,4,3,1,0:T(8,128)(2,1)} %fusion.41, bf16[1,1,4096,1,64]{2,4,3,1,0:T(8,128)(2,1)S(1)} %copy-done.8, bf16[1,1,4096,1,64]{2,4,3,1,0:T(8,128)(2,1)S(1)} %copy-done.11), kind=kOutput, calls=%fused_computation.86 | convolution fusion | flops 1612185600 | bytes 10747904 | tf_op jit(solution)/shard_map/bsd,ibshe->idhe/dot_general | solution.py:70
  (88 shorter events, 7.9 us)
Async XLA Ops:
  7.2 145.9 %copy-start = (bf16[1,4096,1,64]{1,3,2,0:T(8,128)(2,1)S(1)}, bf16[1,4096,1,64]{1,3,2,0:T(8,128)(2,1)}, u32[]{:S(2)}) copy-start(bf16[1,4096,1,64]{1,3,2,0:T(8,128)(2,1)} %param.18) | copy-start | bytes 1572868
  7.2 60.0 %all-gather.5.cloned.1.call-start = ((), (), s32[]{:S(2)}) async-start(), calls=%async_computation.2 | async-start | bytes 8912896 | tf_op jit(solution)/shard_map/all_gather | solution.py:54
  8.0 69.9 %copy-start.16 = (bf16[1024,256]{1,0:T(8,128)(2,1)S(1)}, bf16[1024,256]{1,0:T(8,128)(2,1)}, u32[]{:S(2)}) copy-start(bf16[1024,256]{1,0:T(8,128)(2,1)} %param.28) | copy-start | bytes 1572868
  8.0 138.5 %reduce-scatter.3.cloned.1.call-start = ((), (), s32[]{:S(2)}) async-start(), calls=%async_computation.3 | async-start | bytes 8912896 | tf_op jit(solution)/shard_map/reduce_scatter | solution.py:61
  77.9 68.7 %copy-start.20 = (f32[1024]{0:T(1024)S(1)}, f32[1024]{0:T(1024)}, u32[]{:S(2)}) copy-start(f32[1024]{0:T(1024)} %param.24) | copy-start | bytes 12292
  77.9 68.7 %copy-start.26 = (f32[1024]{0:T(1024)S(1)}, f32[1024]{0:T(1024)}, u32[]{:S(2)}) copy-start(f32[1024]{0:T(1024)} %param.25) | copy-start | bytes 12292
  83.5 66.0 %copy-start.13 = (bf16[1,256,1024]{2,1,0:T(8,128)(2,1)S(1)}, bf16[1,256,1024]{2,1,0:T(8,128)(2,1)}, u32[]{:S(2)}) copy-start(bf16[1,256,1024]{2,1,0:T(8,128)(2,1)} %param.17) | copy-start | bytes 1572868
  83.5 69.6 %copy-start.14 = (bf16[1,4096,1,64]{1,3,2,0:T(8,128)(2,1)S(1)}, bf16[1,4096,1,64]{1,3,2,0:T(8,128)(2,1)}, u32[]{:S(2)}) copy-start(bf16[1,4096,1,64]{1,3,2,0:T(8,128)(2,1)} %param.19) | copy-start | bytes 1572868
  83.5 123.8 %all-gather.7.cloned.1.call-start = ((), (), s32[]{:S(2)}) async-start(), calls=%async_computation.4 | async-start | bytes 8912896 | tf_op jit(solution)/shard_map/all_gather | solution.py:63
  152.6 291.4 %reduce-scatter.5.cloned.1.call-start = ((), (), s32[]{:S(2)}) async-start(), calls=%async_computation.5 | async-start | bytes 8912896 | tf_op jit(solution)/shard_map/reduce_scatter | solution.py:73
  177.0 30.4 %copy-start.19 = (bf16[1,64,1024]{2,1,0:T(8,128)(2,1)S(1)}, bf16[1,64,1024]{2,1,0:T(8,128)(2,1)}, u32[]{:S(2)}) copy-start(bf16[1,64,1024]{2,1,0:T(8,128)(2,1)} %param.27) | copy-start | bytes 393220
  381.1 62.9 %copy-start.21 = (f32[1024]{0:T(1024)S(1)}, f32[1024]{0:T(1024)}, u32[]{:S(2)}) copy-start(f32[1024]{0:T(1024)} %param.22) | copy-start | bytes 12292
  381.1 62.9 %copy-start.27 = (f32[1024]{0:T(1024)S(1)}, f32[1024]{0:T(1024)}, u32[]{:S(2)}) copy-start(f32[1024]{0:T(1024)} %param.23) | copy-start | bytes 12292
  381.1 119.7 %all-gather.11.cloned.1.call-start = ((), (), s32[]{:S(2)}) async-start(), calls=%async_computation.7 | async-start | bytes 8912896 | tf_op jit(solution)/shard_map/all_gather | solution.py:53
  381.8 202.5 %all-gather.9.cloned.1.call-start = ((), (), s32[]{:S(2)}) async-start(), calls=%async_computation.6 | async-start | bytes 8912896 | tf_op jit(solution)/shard_map/all_gather | solution.py:65
  446.5 54.4 %copy-start.2 = (bf16[1,4096,256]{2,1,0:T(8,128)(2,1)S(1)}, bf16[1,4096,256]{2,1,0:T(8,128)(2,1)}, u32[]{:S(2)}) copy-start(bf16[1,4096,256]{2,1,0:T(8,128)(2,1)} %copy-done.1) | copy-start | bytes 6291460
  507.5 30.8 %copy-start.22 = (f32[1024]{0:T(1024)S(1)}, f32[1024]{0:T(1024)}, u32[]{:S(2)}) copy-start(f32[1024]{0:T(1024)} %get-tuple-element.16) | copy-start | bytes 12292
  507.5 30.8 %copy-start.23 = (f32[1024]{0:T(1024)S(1)}, f32[1024]{0:T(1024)}, u32[]{:S(2)}) copy-start(f32[1024]{0:T(1024)} %get-tuple-element.22) | copy-start | bytes 12292
  507.5 30.8 %copy-start.24 = (f32[1024]{0:T(1024)S(1)}, f32[1024]{0:T(1024)}, u32[]{:S(2)}) copy-start(f32[1024]{0:T(1024)} %get-tuple-element.24) | copy-start | bytes 12292
  507.5 30.8 %copy-start.25 = (f32[1024]{0:T(1024)S(1)}, f32[1024]{0:T(1024)}, u32[]{:S(2)}) copy-start(f32[1024]{0:T(1024)} %get-tuple-element.28) | copy-start | bytes 12292
  507.5 75.5 %copy-start.5 = (bf16[1,256,1024]{2,1,0:T(8,128)(2,1)S(1)}, bf16[1,256,1024]{2,1,0:T(8,128)(2,1)}, u32[]{:S(2)}) copy-start(bf16[1,256,1024]{2,1,0:T(8,128)(2,1)} %get-tuple-element.25) | copy-start | bytes 1572868
  507.5 75.5 %copy-start.12 = (bf16[1,256,1024]{2,1,0:T(8,128)(2,1)S(1)}, bf16[1,256,1024]{2,1,0:T(8,128)(2,1)}, u32[]{:S(2)}) copy-start(bf16[1,256,1024]{2,1,0:T(8,128)(2,1)} %reduce-scatter.5.cloned.1.call-done) | copy-start | bytes 1572868
  507.6 76.8 %copy-start.8 = (bf16[1,1,4096,1,64]{2,4,3,1,0:T(8,128)(2,1)S(1)}, bf16[1,1,4096,1,64]{2,4,3,1,0:T(8,128)(2,1)}, u32[]{:S(2)}) copy-start(bf16[1,1,4096,1,64]{2,4,3,1,0:T(8,128)(2,1)} %copy-done.6) | copy-start | bytes 1572868
  507.6 76.7 %copy-start.11 = (bf16[1,1,4096,1,64]{2,4,3,1,0:T(8,128)(2,1)S(1)}, bf16[1,1,4096,1,64]{2,4,3,1,0:T(8,128)(2,1)}, u32[]{:S(2)}) copy-start(bf16[1,1,4096,1,64]{2,4,3,1,0:T(8,128)(2,1)} %copy-done.9) | copy-start | bytes 1572868
  (12 other events, 121.2 us)
Sparse Core Ops, SparseCore 0:
  9.7 57.5 all-gather.4
  83.7 62.8 reduce-scatter.2
  152.7 54.5 all-gather.6
  381.3 62.6 reduce-scatter.4
  446.0 54.7 all-gather.10
  502.3 51.1 all-gather.8
where the time goes:
time: 608 us; the launch traced here: 598 us
  waiting for transfers between devices  239 us (39%)
  matrix products  210 us (35%)
  other arithmetic  86.1 us (14%)
  blocking collectives  44.6 us (7%)
  between operations  14.8 us (2%)
    reduce_scatter x1, waiting for transfers between devices, local_backward(): lax.psum_scatter(h2_partial, 'tp', scatter_dimension=1, tiled=True)  62.5 us
    reduce_scatter x1, waiting for transfers between devices, local_backward(): lax.psum_scatter(h1_partial, 'tp', scatter_dimension=1, tiled=True)  61.4 us
    all_gather x1, waiting for transfers between devices, local_backward(): dout_full = lax.all_gather(d_out, 'tp', axis=1, tiled=True)  59.1 us
    convert_element_type x1, other arithmetic, attention_grads(): (attn_probs * (grad_probs - jnp.sum(grad_probs * attn_probs, axis=-1, kee...  53.4 us
    dot_general x1, matrix products, attention_grads(): jnp.einsum('bqhe,bkhe->bhqk', grad_ctx, v_heads, preferred_element_type=j...  48.6 us
    all_gather x1, waiting for transfers between devices, local_backward(): h2_full = lax.all_gather(h2_local, 'tp', axis=1, tiled=True)  45.7 us
    psum x1, blocking collectives, local_backward(): grad_vecs = lax.psum(vec_partial, 'tp')  44.6 us
    dot_general x1, matrix products, local_backward(): jnp.einsum('bshe,bsd->hed', context, mid_full, preferred_element_type=jnp...  30.8 us
  transfers between devices with their start and end apart: 6, of which 5 were waited for; matrix products, arithmetic and copies ran while one was open for 16% of the time, Pallas kernels for 0%

commit v1 on v0

--- a/solution.py
+++ b/solution.py
@@ -1,11 +1,208 @@
-import jax
-import jax.numpy as jnp
+import functools
+import jax, jax.numpy as jnp
 from jax import lax
+from jax.experimental import pallas as pl
+from jax.experimental.pallas import tpu as pltpu
 from jax.sharding import PartitionSpec as P
 
+F32, BF16 = jnp.float32, jnp.bfloat16
+LOG2E = 1.4426950408889634
 LN_EPS = 1e-5
 GELU_COEF = 0.044715
 GELU_SCALE = 0.7978845608028654
+
+
+def dot(a, b):
+    return lax.dot_general(a, b, (((1,), (0,)), ((), ())), preferred_element_type=F32)
+
+
+def attn_fwd_kernel(blk, qT, kT, vT, lse_out, ctx_out, sum_out, k_rows, s_buf):
+    step = pl.program_id(0)
+    dim, seq = kT.shape
+    c = (dim ** -0.5) * LOG2E
+
+    @pl.when(step == 0)
+    def _():
+        def turn(i, _):
+            cols = pl.ds(pl.multiple_of(i * blk, blk), blk)
+            k_rows[cols, :] = kT[:, cols].T
+            return 0
+        lax.fori_loop(0, seq // blk, turn, 0)
+
+    q = qT[...]
+
+    def stats(i, carry, masked):
+        m, l = carry
+        rows = pl.ds(pl.multiple_of(i * blk, blk), blk)
+        s = dot(k_rows[rows, :], q) * c
+        if masked:
+            r = lax.broadcasted_iota(jnp.int32, (blk, blk), 0)
+            col = lax.broadcasted_iota(jnp.int32, (blk, blk), 1)
+            s = jnp.where(r <= col, s, -1e30)
+        s_buf[rows, :] = s
+        new = jnp.maximum(m, jnp.max(s, axis=0, keepdims=True))
+        l = l * jnp.exp2(m - new) + jnp.sum(jnp.exp2(s - new), axis=0, keepdims=True)
+        return new, l
+
+    init = (jnp.full((1, blk), -1e30, F32), jnp.zeros((1, blk), F32))
+    carry = lax.fori_loop(0, step, functools.partial(stats, masked=False), init)
+    m, l = stats(step, carry, True)
+    lse = m + jnp.log2(l)
+
+    def apply(i, carry):
+        low_sum, res_sum = carry
+        rows = pl.ds(pl.multiple_of(i * blk, blk), blk)
+        p = jnp.exp2(s_buf[rows, :] - lse)
+        low = p.astype(BF16)
+        res = (p - low.astype(F32)).astype(BF16)
+        v = vT[:, rows]
+        return low_sum + dot(v, low), res_sum + dot(v, res)
+
+    zero = jnp.zeros((dim, blk), F32)
+    low_sum, res_sum = lax.fori_loop(0, step + 1, apply, (zero, zero))
+    ctx_out[...] = low_sum.astype(BF16)
+    sum_out[...] = low_sum + res_sum
+    lse_out[...] = jnp.broadcast_to(lse, (8, blk))
+
+
+def attn_fwd(qT, kT, vT, blk=1024):
+    dim, seq = qT.shape
+    col = lambda i: (0, i)
+    full = lambda i: (0, 0)
+    return pl.pallas_call(
+        functools.partial(attn_fwd_kernel, blk),
+        grid=(seq // blk,),
+        in_specs=[pl.BlockSpec((dim, blk), col), pl.BlockSpec((dim, seq), full), pl.BlockSpec((dim, seq), full)],
+        out_specs=[pl.BlockSpec((8, blk), col), pl.BlockSpec((dim, blk), col), pl.BlockSpec((dim, blk), col)],
+        out_shape=[jax.ShapeDtypeStruct((8, seq), F32), jax.ShapeDtypeStruct((dim, seq), BF16), jax.ShapeDtypeStruct((dim, seq), F32)],
+        scratch_shapes=[pltpu.VMEM((seq, dim), BF16), pltpu.VMEM((seq, blk), F32)],
+        compiler_params=pltpu.CompilerParams(dimension_semantics=("arbitrary",), vmem_limit_bytes=32 << 20),
+        cost_estimate=pl.CostEstimate(flops=3 * seq * seq * 256, bytes_accessed=8 * dim * seq, transcendentals=seq * seq),
+        name="attn_fwd",
+    )(qT, kT, vT)
+
+
+def attn_bwd_kernel(blk, qT, kT, vT, dctxT, lse, ctxsum, out, k_rows, dk_acc, dv_acc):
+    step = pl.program_id(0)
+    last = pl.num_programs(0) - 1
+    dim, seq = kT.shape
+    scale = dim ** -0.5
+    c = scale * LOG2E
+
+    @pl.when(step == 0)
+    def _():
+        def turn(i, _):
+            cols = pl.ds(pl.multiple_of(i * blk, blk), blk)
+            k_rows[cols, :] = kT[:, cols].T
+            dk_acc[:, cols] = jnp.zeros((dim, blk), F32)
+            dv_acc[:, cols] = jnp.zeros((dim, blk), F32)
+            return 0
+        lax.fori_loop(0, seq // blk, turn, 0)
+
+    qt = qT[...]
+    dct = dctxT[...]
+    q = qt.T
+    dc = dct.T
+    delta_row = jnp.sum(dct.astype(F32) * ctxsum[...], axis=0, keepdims=True)
+    lse_col = jnp.broadcast_to(lse[0:1, :], (128, blk)).T[:, :1]
+    delta_col = jnp.broadcast_to(delta_row, (128, blk)).T[:, :1]
+
+    def block(i, dq, masked):
+        cols = pl.ds(pl.multiple_of(i * blk, blk), blk)
+        s = dot(q, kT[:, cols]) * c
+        dp = dot(dc, vT[:, cols])
+        p = jnp.exp2(s - lse_col)
+        if masked:
+            r = lax.broadcasted_iota(jnp.int32, (blk, blk), 0)
+            col = lax.broadcasted_iota(jnp.int32, (blk, blk), 1)
+            p = jnp.where(r >= col, p, 0.0)
+        ds = (p * (dp - delta_col)).astype(BF16)
+        dv_acc[:, cols] += dot(dct, p.astype(BF16))
+        dk_acc[:, cols] += dot(qt, ds)
+        return dq + dot(ds, k_rows[cols, :])
+
+    dq = lax.fori_loop(0, step, functools.partial(block, masked=False), jnp.zeros((blk, dim), F32))
+    dq = block(step, dq, True)
+    out[0:dim, pl.ds(pl.multiple_of(step * blk, blk), blk)] = (dq * scale).T.astype(BF16)
+
+    @pl.when(step == last)
+    def _():
+        def put(i, _):
+            cols = pl.ds(pl.multiple_of(i * blk, blk), blk)
+            out[dim:2 * dim, cols] = (dk_acc[:, cols] * scale).astype(BF16)
+            out[2 * dim:3 * dim, cols] = dv_acc[:, cols].astype(BF16)
+            return 0
+        lax.fori_loop(0, seq // blk, put, 0)
+
+
+def attn_bwd(qT, kT, vT, dctxT, lse, ctxsum, blk=512):
+    dim, seq = qT.shape
+    col = lambda i: (0, i)
+    full = lambda i: (0, 0)
+    return pl.pallas_call(
+        functools.partial(attn_bwd_kernel, blk),
+        grid=(seq // blk,),
+        in_specs=[pl.BlockSpec((dim, blk), col), pl.BlockSpec((dim, seq), full), pl.BlockSpec((dim, seq), full),
+                  pl.BlockSpec((dim, blk), col), pl.BlockSpec((8, blk), col), pl.BlockSpec((dim, blk), col)],
+        out_specs=pl.BlockSpec((3 * dim, seq), full),
+        out_shape=jax.ShapeDtypeStruct((3 * dim, seq), BF16),
+        scratch_shapes=[pltpu.VMEM((seq, dim), BF16), pltpu.VMEM((dim, seq), F32), pltpu.VMEM((dim, seq), F32)],
+        compiler_params=pltpu.CompilerParams(dimension_semantics=("arbitrary",), vmem_limit_bytes=40 << 20),
+        cost_estimate=pl.CostEstimate(flops=5 * seq * seq * 256, bytes_accessed=14 * dim * seq, transcendentals=seq * seq // 2),
+        name="attn_bwd",
+    )(qT, kT, vT, dctxT, lse, ctxsum)
+
+
+def vec_sum_kernel(n, part, out, buf, send_sem, recv_sem):
+    me = lax.axis_index('tp')
+    barrier = pltpu.get_barrier_semaphore()
+
+    def hello(r, _):
+        pl.semaphore_signal(barrier, inc=1, device_id={'tp': lax.rem(me + r, n)}, device_id_type=pl.DeviceIdType.MESH)
+        return 0
+    lax.fori_loop(1, n, hello, 0)
+    pl.semaphore_wait(barrier, n - 1)
+
+    def copy(r):
+        return pltpu.make_async_remote_copy(
+            src_ref=part, dst_ref=buf.at[me], send_sem=send_sem.at[r], recv_sem=recv_sem.at[me],
+            device_id={'tp': lax.rem(me + r, n)}, device_id_type=pl.DeviceIdType.MESH)
+
+    def arrived(r):
+        src = lax.rem(me + n - r, n)
+        return pltpu.make_async_remote_copy(
+            src_ref=part, dst_ref=buf.at[src], send_sem=send_sem.at[r], recv_sem=recv_sem.at[src],
+            device_id={'tp': src}, device_id_type=pl.DeviceIdType.MESH)
+
+    def send(r, _):
+        copy(r).start()
+        return 0
+    lax.fori_loop(1, n, send, 0)
+    buf[pl.ds(me, 1)] = part[...][None]
+
+    def wait(r, _):
+        arrived(r).wait_recv()
+        return 0
+    lax.fori_loop(1, n, wait, 0)
+    out[...] = lax.fori_loop(1, n, lambda j, acc: acc + buf[j], buf[0])
+
+    def drain(r, _):
+        copy(r).wait_send()
+        return 0
+    lax.fori_loop(1, n, drain, 0)
+
+
+def vec_sum(part, n):
+    rows, width = part.shape
+    return pl.pallas_call(
+        functools.partial(vec_sum_kernel, n),
+        in_specs=[pl.BlockSpec(memory_space=pltpu.VMEM)],
+        out_specs=pl.BlockSpec(memory_space=pltpu.VMEM),
+        out_shape=jax.ShapeDtypeStruct((rows, width), F32),
+        scratch_shapes=[pltpu.VMEM((n, rows, width), F32), pltpu.SemaphoreType.DMA((n,)), pltpu.SemaphoreType.DMA((n,))],
+        compiler_params=pltpu.CompilerParams(collective_id=1, has_side_effects=True),
+        name="vec_sum",
+    )(part)
 
 
 def layer_norm_fwd(token_rows, norm_gain, norm_bias):
@@ -27,24 +224,6 @@
     act_value = 0.5 * pre_act * (1.0 + tanh_val)
     act_slope = 0.5 * (1.0 + tanh_val) + 0.5 * pre_act * (1.0 - tanh_val * tanh_val) * GELU_SCALE * (1.0 + 3.0 * GELU_COEF * pre_act * pre_act)
     return act_value, act_slope
-
-
-def attention_grads(q_heads, k_heads, v_heads, grad_ctx):
-    seq_len = q_heads.shape[1]
-    score_scale = q_heads.shape[-1] ** -0.5
-    scores = jnp.einsum('bqhe,bkhe->bhqk', q_heads, k_heads, preferred_element_type=jnp.float32) * score_scale
-    row_ids = lax.broadcasted_iota(jnp.int32, (seq_len, seq_len), 0)
-    col_ids = lax.broadcasted_iota(jnp.int32, (seq_len, seq_len), 1)
-    scores = jnp.where(row_ids >= col_ids, scores, -1e30)
-    attn_probs = jax.nn.softmax(scores, axis=-1)
-    probs_low = attn_probs.astype(jnp.bfloat16)
-    context = jnp.einsum('bhqk,bkhe->bqhe', probs_low, v_heads, preferred_element_type=jnp.float32).astype(jnp.bfloat16)
-    grad_probs = jnp.einsum('bqhe,bkhe->bhqk', grad_ctx, v_heads, preferred_element_type=jnp.float32)
-    grad_scores = (attn_probs * (grad_probs - jnp.sum(grad_probs * attn_probs, axis=-1, keepdims=True)) * score_scale).astype(jnp.bfloat16)
-    grad_q = jnp.einsum('bhqk,bkhe->bqhe', grad_scores, k_heads, preferred_element_type=jnp.float32).astype(jnp.bfloat16)
-    grad_k = jnp.einsum('bhqk,bqhe->bkhe', grad_scores, q_heads, preferred_element_type=jnp.float32).astype(jnp.bfloat16)
-    grad_v = jnp.einsum('bhqk,bqhe->bkhe', probs_low, grad_ctx, preferred_element_type=jnp.float32).astype(jnp.bfloat16)
-    return context, grad_q, grad_k, grad_v
 
 
 def solution(mesh):
@@ -63,13 +242,18 @@
         mid_full = lax.all_gather(grad_mid, 'tp', axis=1, tiled=True)
         norm1_hat, norm1_rstd, h1_local = layer_norm_fwd(x_in, ln1_gain, ln1_bias)
         h1_full = lax.all_gather(h1_local, 'tp', axis=1, tiled=True)
-        grad_ctx = jnp.einsum('bsd,hed->bshe', mid_full, w_proj, preferred_element_type=jnp.float32).astype(jnp.bfloat16)
-        context, grad_q, grad_k, grad_v = attention_grads(q_saved, k_saved, v_saved, grad_ctx)
-        grad_wproj = jnp.einsum('bshe,bsd->hed', context, mid_full, preferred_element_type=jnp.float32)
-        qkv_grads = jnp.stack([grad_q, grad_k, grad_v])
-        grad_wqkv = jnp.einsum('bsd,ibshe->idhe', h1_full, qkv_grads, preferred_element_type=jnp.float32)
-        grad_bqkv = jnp.sum(qkv_grads, axis=(1, 2), dtype=jnp.float32)
-        h1_partial = jnp.einsum('ibshe,idhe->bsd', qkv_grads, w_qkv, preferred_element_type=jnp.float32).astype(jnp.bfloat16)
+        dim = q_saved.shape[-1]
+        seq = q_saved.shape[1]
+        q_t, k_t, v_t = (jnp.transpose(a[0, :, 0, :]) for a in (q_saved, k_saved, v_saved))
+        lse, ctx_t, ctx_sum = attn_fwd(q_t, k_t, v_t)
+        dctx_t = jnp.einsum('ed,sd->es', w_proj[0], mid_full[0], preferred_element_type=jnp.float32).astype(jnp.bfloat16)
+        dqkv_t = attn_bwd(q_t, k_t, v_t, dctx_t, lse, ctx_sum)
+        grad_wproj = jnp.einsum('es,sd->ed', ctx_t, mid_full[0], preferred_element_type=jnp.float32)[None]
+        w_qkv_t = jnp.transpose(w_qkv[:, :, 0, :], (0, 2, 1)).reshape(3 * dim, -1)
+        grad_w_t = jnp.einsum('es,sd->ed', dqkv_t, h1_full[0], preferred_element_type=jnp.float32)
+        grad_wqkv = jnp.transpose(grad_w_t.reshape(3, dim, -1), (0, 2, 1))[:, :, None, :]
+        grad_bqkv = jnp.sum(dqkv_t, axis=1, dtype=jnp.float32).reshape(3, 1, dim)
+        h1_partial = jnp.einsum('es,ed->sd', dqkv_t, w_qkv_t, preferred_element_type=jnp.float32).astype(jnp.bfloat16)[None]
         grad_h1 = lax.psum_scatter(h1_partial, 'tp', scatter_dimension=1, tiled=True).astype(jnp.float32)
         grad_x = (grad_mid.astype(jnp.float32) + layer_norm_bwd(grad_h1, norm1_hat, norm1_rstd, ln1_gain)).astype(jnp.bfloat16)
         vec_partial = jnp.stack([
@@ -80,7 +264,7 @@
             jnp.sum(grad_mid, axis=(0, 1), dtype=jnp.float32),
             jnp.sum(d_out, axis=(0, 1), dtype=jnp.float32),
         ])
-        grad_vecs = lax.psum(vec_partial, 'tp')
+        grad_vecs = vec_sum(vec_partial, mesh.shape['tp'])
         return grad_x, grad_wqkv, grad_bqkv, grad_wproj, grad_wfc1, grad_bfc1, grad_wfc2, grad_vecs
 
     tok_spec = P('dp', 'tp', None)

time: 608 us -> 448 us (0.74); the launches traced: 598 us -> 448 us
  matrix products: 210 us -> 53.3 us
  Pallas kernels: 0 us -> 82.8 us
  other arithmetic: 86.1 us -> 9.64 us
  blocking collectives: 44.6 us -> 0 us
  waiting for transfers between devices: 239 us -> 281 us
    dot_general x9 -> x4, matrix products: 180 us -> 23.5 us  [the longest x1 6.13 us: local_backward(): jnp.einsum('es,sd->ed', dqkv_t, h1_full[0], preferred_element_type=jnp.fl...]
    pallas_call x0 -> x3, Pallas kernels: none -> 82.8 us  [the longest x1 31.7 us: attn_bwd(): pl.pallas_call(functools.partial(attn_bwd_kernel, blk), grid=(seq // blk,...]
    convert_element_type x1 -> x0, other arithmetic: 53.4 us -> none  [attention_grads(): (attn_probs * (grad_probs - jnp.sum(grad_probs * attn_probs, axis=-1, kee...]
    psum x1 -> x0, blocking collectives: 44.6 us -> none  [local_backward(): grad_vecs = lax.psum(vec_partial, 'tp')]
    all_gather x1, waiting for transfers between devices: 0.01 us -> 29.5 us  [local_backward(): h1_full = lax.all_gather(h1_local, 'tp', axis=1, tiled=True)]
    reduce_sum x2 -> x1, other arithmetic: 22.1 us -> 0.29 us  [local_backward(): grad_bqkv = jnp.sum(dqkv_t, axis=1, dtype=jnp.float32).reshape(3, 1, dim)]
    all_gather x1, waiting for transfers between devices: 8.57 us -> 28.3 us  [local_backward(): mid_full = lax.all_gather(grad_mid, 'tp', axis=1, tiled=True)]
  transfers between devices with their start and end apart: 6 -> 6, of which waited for: 5 -> 6; matrix products, arithmetic and copies ran while one was open for 16% -> 6% of each run, Pallas kernels for 0% -> 11%
where the time goes in v1:
time: 448 us
  waiting for transfers between devices  281 us (63%)
  Pallas kernels  82.8 us (18%)
  matrix products  53.3 us (12%)
  between operations  14.3 us (3%)
  other arithmetic  9.64 us (2%)
  local copies, waits for them, and re-layouts  5.43 us (1%)
    reduce_scatter x1, waiting for transfers between devices, local_backward(): lax.psum_scatter(h2_partial, 'tp', scatter_dimension=1, tiled=True)  61.4 us
    reduce_scatter x1, waiting for transfers between devices, local_backward(): lax.psum_scatter(h1_partial, 'tp', scatter_dimension=1, tiled=True)  61.4 us
    all_gather x1, waiting for transfers between devices, local_backward(): dout_full = lax.all_gather(d_out, 'tp', axis=1, tiled=True)  59.1 us
    all_gather x1, waiting for transfers between devices, local_backward(): h2_full = lax.all_gather(h2_local, 'tp', axis=1, tiled=True)  40.1 us
    pallas_call x1, Pallas kernels, attn_bwd(): pl.pallas_call(functools.partial(attn_bwd_kernel, blk), grid=(seq // blk,...  31.7 us
    all_gather x1, waiting for transfers between devices, local_backward(): h1_full = lax.all_gather(h1_local, 'tp', axis=1, tiled=True)  29.5 us
    all_gather x1, waiting for transfers between devices, local_backward(): mid_full = lax.all_gather(grad_mid, 'tp', axis=1, tiled=True)  28.3 us
    pallas_call x1, Pallas kernels, attn_fwd(): pl.pallas_call(functools.partial(attn_fwd_kernel, blk), grid=(seq // blk,...  26.1 us
  transfers between devices with their start and end apart: 6, of which 6 were waited for; matrix products, arithmetic and copies ran while one was open for 6% of the time, Pallas kernels for 11%

profile of v1, /device:TPU:21, one launch (start us, length us, event | category | flops | bytes accessed | tf_op | source)
XLA Modules:
  0.0 447.6 jit_solution(4907371683702760545)
XLA Ops:
  8.1 59.1 %all-gather.5.cloned.1.call-done = bf16[1,4096,1024]{2,1,0:T(8,128)(2,1)} async-done(((bf16[1,256,1024]{2,1,0:T(8,128)(2,1)}), bf16[1,4096,1024]{2,1,0:T(8,128)(2,1)}) %all-gather.5.cloned.1.call-update) | async-done | bytes 8388624 | tf_op jit(solution)/shard_map/all_gather | solution.py:233
  67.2 9.4 %convert_reduce_fusion = (f32[256]{0:T(256)}, bf16[1,4096,256]{2,1,0:T(8,128)(2,1)S(1)}) fusion(bf16[1,4096,256]{2,1,0:T(8,128)(2,1)} %param.21, bf16[256,1024]{1,0:T(8,128)(2,1)} %param.29, bf16[1,4096,1024]{2,1,0:T(8,128)(2,1)} %all-gather.5.cloned.1.call-done), kind=kOutput, calls=%fused_computation.35 | convolution fusion | flops 2170552064 | bytes 13108224 | tf_op jit(solution)/shard_map/bsd,fd->bsf/dot_general | solution.py:236
  76.6 1.3 copy-done.8
  77.9 5.6 %convert_bitcast_fusion.1 = bf16[1,4096,1024]{2,1,0:T(8,128)(2,1)} fusion(bf16[1024,256]{1,0:T(8,128)(2,1)S(1)} %copy-done, bf16[1,4096,256]{2,1,0:T(8,128)(2,1)S(1)} %get-tuple-element.36), kind=kOutput, calls=%fused_computation.20 | convolution fusion | flops 2151677952 | bytes 11010048 | tf_op jit(solution)/shard_map/bsf,df->bsd/dot_general | solution.py:239
  83.6 0.9 copy-done.9
  85.0 61.4 %reduce-scatter.3.cloned.1.call-done = bf16[1,256,1024]{2,1,0:T(8,128)(2,1)} async-done(((bf16[1,4096,1024]{2,1,0:T(8,128)(2,1)}), bf16[1,256,1024]{2,1,0:T(8,128)(2,1)}) %reduce-scatter.3.cloned.1.call-update) | async-done | bytes 524304 | tf_op jit(solution)/shard_map/reduce_scatter | solution.py:240
  146.4 2.4 fusion.78
  148.8 2.4 convert_reduce_fusion.5
  151.6 26.1 %attn_fwd.1 = (f32[8,4096]{1,0:T(8,128)S(1)}, bf16[64,4096]{1,0:T(8,128)(2,1)S(1)}, f32[64,4096]{1,0:T(8,128)S(1)}) custom-call(bf16[64,4096]{1,0:T(8,128)(2,1)S(1)} %bitcast.92, bf16[64,4096]{1,0:T(8,128)(2,1)S(1)} %bitcast.94, bf16[64,4096]{1,0:T(8,128)(2,1)S(1)} %bitcast.96), custom_call_target="tpu_custom_call" | custom-call | flops 12884901888 | bytes 2097152 | tf_op jit(solution)/shard_map/attn_fwd/pallas_call | solution.py:72
  177.6 28.3 %all-gather.7.cloned.1.call-done = bf16[1,4096,1024]{2,1,0:T(8,128)(2,1)} async-done(((bf16[1,256,1024]{2,1,0:T(8,128)(2,1)}), bf16[1,4096,1024]{2,1,0:T(8,128)(2,1)}) %all-gather.7.cloned.1.call-update) | async-done | bytes 8388624 | tf_op jit(solution)/shard_map/all_gather | solution.py:242
  206.0 6.1 %fusion.26.dctxT = bf16[64,4096]{1,0:T(8,128)(2,1)S(1)} fusion(bf16[1,4096,1024]{2,1,0:T(8,128)(2,1)} %all-gather.7.cloned.1.call-done, bf16[1,64,1024]{2,1,0:T(8,128)(2,1)S(1)} %copy-done.15), kind=kOutput, calls=%fused_computation.27 | convolution fusion | flops 537133056 | bytes 9043968 | tf_op jit(solution)/shard_map/ed,sd->es/dot_general | solution.py:249
  212.1 1.2 copy-done.7
  213.3 31.7 %attn_bwd.1 = bf16[192,4096]{1,0:T(8,128)(2,1)S(1)} custom-call(bf16[64,4096]{1,0:T(8,128)(2,1)S(1)} %bitcast.93, bf16[64,4096]{1,0:T(8,128)(2,1)S(1)} %bitcast.95, bf16[64,4096]{1,0:T(8,128)(2,1)S(1)} %bitcast.97, bf16[64,4096]{1,0:T(8,128)(2,1)S(1)} %fusion.26.dctxT, f32[8,4096]{1,0:T(8,128)S(1)} %get-tuple-element.11.lse, f32[64,4096]{1,0:T(8,128)S(1)} %copy-done.7), custom_call_target="tpu_custom_call" | custom-call | flops 21474836480 | bytes 3670016 | tf_op jit(solution)/shard_map/attn_bwd/pallas_call | solution.py:142
  245.0 5.6 %convert_bitcast_fusion = bf16[1,4096,1024]{2,1,0:T(8,128)(2,1)} fusion(bf16[192,4096]{1,0:T(8,128)(2,1)S(1)} %attn_bwd.1, bf16[192,1024]{1,0:T(8,128)(2,1)S(1)} %bitcast.98), kind=kOutput, calls=%fused_computation.19 | convolution fusion | flops 1614807040 | bytes 10354688 | tf_op jit(solution)/shard_map/es,ed->sd/dot_general | solution.py:256
  252.1 61.4 %reduce-scatter.5.cloned.1.call-done = bf16[1,256,1024]{2,1,0:T(8,128)(2,1)} async-done(((bf16[1,4096,1024]{2,1,0:T(8,128)(2,1)}), bf16[1,256,1024]{2,1,0:T(8,128)(2,1)}) %reduce-scatter.5.cloned.1.call-update) | async-done | bytes 524304 | tf_op jit(solution)/shard_map/reduce_scatter | solution.py:257
  313.5 2.4 fusion.79
  315.9 7.6 %fusion.8 = f32[256,1024]{1,0:T(8,128)} fusion(bf16[1,4096,1024]{2,1,0:T(8,128)(2,1)} %all-gather.5.cloned.1.call-done, bf16[1,4096,256]{2,1,0:T(8,128)(2,1)} %param.21), kind=kOutput, calls=%fused_computation.15 | convolution fusion | flops 2157969408 | bytes 11534336 | tf_op jit(solution)/shard_map/bsf,bsd->fd/dot_general | solution.py:235
  324.5 5.7 %fusion.61 = f32[1,64,1024]{2,1,0:T(8,128)} fusion(bf16[64,4096]{1,0:T(8,128)(2,1)S(1)} %get-tuple-element.13, bf16[1,4096,1024]{2,1,0:T(8,128)(2,1)} %all-gather.7.cloned.1.call-done), kind=kOutput, calls=%fused_computation.73 | convolution fusion | flops 536870912 | bytes 9175040 | tf_op jit(solution)/shard_map/es,sd->ed/dot_general | solution.py:251
  330.1 40.1 %all-gather.11.cloned.1.call-done = bf16[1,4096,1024]{2,1,0:T(8,128)(2,1)} async-done(((bf16[1,256,1024]{2,1,0:T(8,128)(2,1)}), bf16[1,4096,1024]{2,1,0:T(8,128)(2,1)}) %all-gather.11.cloned.1.call-update) | async-done | bytes 8388624 | tf_op jit(solution)/shard_map/all_gather | solution.py:232
  370.2 7.3 %fusion = f32[1024,256]{1,0:T(8,128)} fusion(bf16[1,4096,1024]{2,1,0:T(8,128)(2,1)} %all-gather.11.cloned.1.call-done, bf16[1,4096,256]{2,1,0:T(8,128)(2,1)} %copy-done.8), kind=kOutput, calls=%fused_computation.7 | convolution fusion | flops 2147483648 | bytes 11534336 | tf_op jit(solution)/shard_map/bsd,bsf->df/dot_general | solution.py:237
  378.2 25.1 %vec_sum.1 = f32[6,1024]{1,0:T(8,128)} custom-call(f32[6,1024]{1,0:T(8,128)} %stack.27.part), custom_call_target="tpu_custom_call" | custom-call | tf_op jit(solution)/shard_map/vec_sum/pallas_call | solution.py:197
  403.3 1.3 fusion.75
  404.6 29.5 %all-gather.9.cloned.1.call-done = bf16[1,4096,1024]{2,1,0:T(8,128)(2,1)} async-done(((bf16[1,256,1024]{2,1,0:T(8,128)(2,1)}), bf16[1,4096,1024]{2,1,0:T(8,128)(2,1)}) %all-gather.9.cloned.1.call-update) | async-done | bytes 8388624 | tf_op jit(solution)/shard_map/all_gather | solution.py:244
  434.0 6.1 %fusion.50 = f32[3,1024,1,64]{1,3,2,0:T(8,128)} fusion(bf16[3,64,4096]{2,1,0:T(8,128)(2,1)S(1)} %bitcast.91, bf16[1,4096,1024]{2,1,0:T(8,128)(2,1)} %all-gather.9.cloned.1.call-done), kind=kOutput, calls=%fused_computation.64 | convolution fusion | flops 1610612736 | bytes 10747904 | tf_op jit(solution)/shard_map/es,sd->ed/dot_general | solution.py:253
  (66 shorter events, 5.5 us)
Async XLA Ops:
  7.2 70.7 %copy-start = (bf16[1024,256]{1,0:T(8,128)(2,1)S(1)}, bf16[1024,256]{1,0:T(8,128)(2,1)}, u32[]{:S(2)}) copy-start(bf16[1024,256]{1,0:T(8,128)(2,1)} %param.28) | copy-start | bytes 1572868
  7.2 60.0 %all-gather.5.cloned.1.call-start = ((), (), s32[]{:S(2)}) async-start(), calls=%async_computation.2 | async-start | bytes 8912896 | tf_op jit(solution)/shard_map/all_gather | solution.py:233
  8.0 138.4 %reduce-scatter.3.cloned.1.call-start = ((), (), s32[]{:S(2)}) async-start(), calls=%async_computation.3 | async-start | bytes 8912896 | tf_op jit(solution)/shard_map/reduce_scatter | solution.py:240
  76.6 1.3 copy-start.8
  83.5 62.9 %copy-start.17 = (f32[1024]{0:T(1024)S(1)}, f32[1024]{0:T(1024)}, u32[]{:S(2)}) copy-start(f32[1024]{0:T(1024)} %param.24) | copy-start | bytes 12292
  83.5 62.9 %copy-start.19 = (f32[1024]{0:T(1024)S(1)}, f32[1024]{0:T(1024)}, u32[]{:S(2)}) copy-start(f32[1024]{0:T(1024)} %param.25) | copy-start | bytes 12292
  83.5 65.3 %copy-start.13 = (bf16[1,256,1024]{2,1,0:T(8,128)(2,1)S(1)}, bf16[1,256,1024]{2,1,0:T(8,128)(2,1)}, u32[]{:S(2)}) copy-start(bf16[1,256,1024]{2,1,0:T(8,128)(2,1)} %param.17) | copy-start | bytes 1572868
  83.5 68.0 %copy-start.2 = (bf16[1,4096,1,64]{1,3,2,0:T(8,128)(2,1)S(1)}, bf16[1,4096,1,64]{1,3,2,0:T(8,128)(2,1)}, u32[]{:S(2)}) copy-start(bf16[1,4096,1,64]{1,3,2,0:T(8,128)(2,1)} %param.18) | copy-start | bytes 1572868
  83.5 68.0 %copy-start.3 = (bf16[1,4096,1,64]{1,3,2,0:T(8,128)(2,1)S(1)}, bf16[1,4096,1,64]{1,3,2,0:T(8,128)(2,1)}, u32[]{:S(2)}) copy-start(bf16[1,4096,1,64]{1,3,2,0:T(8,128)(2,1)} %param.19) | copy-start | bytes 1572868
  83.6 68.0 %copy-start.4 = (bf16[1,4096,1,64]{1,3,2,0:T(8,128)(2,1)S(1)}, bf16[1,4096,1,64]{1,3,2,0:T(8,128)(2,1)}, u32[]{:S(2)}) copy-start(bf16[1,4096,1,64]{1,3,2,0:T(8,128)(2,1)} %param.20) | copy-start | bytes 1572868
  83.6 122.4 %all-gather.7.cloned.1.call-start = ((), (), s32[]{:S(2)}) async-start(), calls=%async_computation.4 | async-start | bytes 8912896 | tf_op jit(solution)/shard_map/all_gather | solution.py:242
  151.3 162.2 %reduce-scatter.5.cloned.1.call-start = ((), (), s32[]{:S(2)}) async-start(), calls=%async_computation.5 | async-start | bytes 8912896 | tf_op jit(solution)/shard_map/reduce_scatter | solution.py:257
  151.5 54.4 %copy-start.15 = (bf16[1,64,1024]{2,1,0:T(8,128)(2,1)S(1)}, bf16[1,64,1024]{2,1,0:T(8,128)(2,1)}, u32[]{:S(2)}) copy-start(bf16[1,64,1024]{2,1,0:T(8,128)(2,1)} %param.27) | copy-start | bytes 393220
  177.6 34.4 %copy-start.6 = (f32[64,4096]{1,0:T(8,128)}, f32[64,4096]{1,0:T(8,128)S(1)}, u32[]{:S(2)}) copy-start(f32[64,4096]{1,0:T(8,128)S(1)} %get-tuple-element.12.ctxsum) | copy-start | bytes 3145732
  206.0 6.1 %copy-start.5 = (bf16[1,4096,1,64]{1,3,2,0:T(8,128)(2,1)S(1)}, bf16[1,4096,1,64]{1,3,2,0:T(8,128)(2,1)}, u32[]{:S(2)}) copy-start(bf16[1,4096,1,64]{1,3,2,0:T(8,128)(2,1)} %param.20) | copy-start | bytes 1572868
  213.3 31.7 %copy-start.14 = (bf16[3,1024,1,64]{1,3,2,0:T(8,128)(2,1)S(1)}, bf16[3,1024,1,64]{1,3,2,0:T(8,128)(2,1)}, u32[]{:S(2)}) copy-start(bf16[3,1024,1,64]{1,3,2,0:T(8,128)(2,1)} %param.26) | copy-start | bytes 1179652
  250.6 62.9 %copy-start.18 = (f32[1024]{0:T(1024)S(1)}, f32[1024]{0:T(1024)}, u32[]{:S(2)}) copy-start(f32[1024]{0:T(1024)} %param.22) | copy-start | bytes 12292
  250.6 62.9 %copy-start.20 = (f32[1024]{0:T(1024)S(1)}, f32[1024]{0:T(1024)}, u32[]{:S(2)}) copy-start(f32[1024]{0:T(1024)} %param.23) | copy-start | bytes 12292
  250.7 119.5 %all-gather.11.cloned.1.call-start = ((), (), s32[]{:S(2)}) async-start(), calls=%async_computation.7 | async-start | bytes 8912896 | tf_op jit(solution)/shard_map/all_gather | solution.py:232
  251.4 182.7 %all-gather.9.cloned.1.call-start = ((), (), s32[]{:S(2)}) async-start(), calls=%async_computation.6 | async-start | bytes 8912896 | tf_op jit(solution)/shard_map/all_gather | solution.py:244
  330.1 73.2 %copy-start.11 = (bf16[1,256,1024]{2,1,0:T(8,128)(2,1)S(1)}, bf16[1,256,1024]{2,1,0:T(8,128)(2,1)}, u32[]{:S(2)}) copy-start(bf16[1,256,1024]{2,1,0:T(8,128)(2,1)} %get-tuple-element.31) | copy-start | bytes 1572868
  330.1 73.2 %copy-start.12 = (bf16[1,256,1024]{2,1,0:T(8,128)(2,1)S(1)}, bf16[1,256,1024]{2,1,0:T(8,128)(2,1)}, u32[]{:S(2)}) copy-start(bf16[1,256,1024]{2,1,0:T(8,128)(2,1)} %reduce-scatter.5.cloned.1.call-done) | copy-start | bytes 1572868
  434.0 6.8 %copy-start.1 = (bf16[1024,256]{1,0:T(8,128)(2,1)S(1)}, bf16[1024,256]{1,0:T(8,128)(2,1)}, u32[]{:S(2)}) copy-start(bf16[1024,256]{1,0:T(8,128)(2,1)} %param.28) | copy-start | bytes 1572868
  434.0 6.1 %copy-start.16 = (f32[6,1024]{1,0:T(8,128)S(1)}, f32[6,1024]{1,0:T(8,128)}, u32[]{:S(2)}) copy-start(f32[6,1024]{1,0:T(8,128)} %vec_sum.1) | copy-start | bytes 73732
  (3 other events, 3.3 us)
Sparse Core Ops, SparseCore 0:
  9.7 57.5 all-gather.4
  83.7 62.6 reduce-scatter.2
  151.4 54.5 all-gather.6
  250.8 62.6 reduce-scatter.4
  315.5 54.6 all-gather.10
  371.7 62.2 all-gather.8

commit v2 on v1

--- a/solution.py
+++ b/solution.py
@@ -153,58 +153,6 @@
     )(qT, kT, vT, dctxT, lse, ctxsum)
 
 
-def vec_sum_kernel(n, part, out, buf, send_sem, recv_sem):
-    me = lax.axis_index('tp')
-    barrier = pltpu.get_barrier_semaphore()
-
-    def hello(r, _):
-        pl.semaphore_signal(barrier, inc=1, device_id={'tp': lax.rem(me + r, n)}, device_id_type=pl.DeviceIdType.MESH)
-        return 0
-    lax.fori_loop(1, n, hello, 0)
-    pl.semaphore_wait(barrier, n - 1)
-
-    def copy(r):
-        return pltpu.make_async_remote_copy(
-            src_ref=part, dst_ref=buf.at[me], send_sem=send_sem.at[r], recv_sem=recv_sem.at[me],
-            device_id={'tp': lax.rem(me + r, n)}, device_id_type=pl.DeviceIdType.MESH)
-
-    def arrived(r):
-        src = lax.rem(me + n - r, n)
-        return pltpu.make_async_remote_copy(
-            src_ref=part, dst_ref=buf.at[src], send_sem=send_sem.at[r], recv_sem=recv_sem.at[src],
-            device_id={'tp': src}, device_id_type=pl.DeviceIdType.MESH)
-
-    def send(r, _):
-        copy(r).start()
-        return 0
-    lax.fori_loop(1, n, send, 0)
-    buf[pl.ds(me, 1)] = part[...][None]
-
-    def wait(r, _):
-        arrived(r).wait_recv()
-        return 0
-    lax.fori_loop(1, n, wait, 0)
-    out[...] = lax.fori_loop(1, n, lambda j, acc: acc + buf[j], buf[0])
-
-    def drain(r, _):
-        copy(r).wait_send()
-        return 0
-    lax.fori_loop(1, n, drain, 0)
-
-
-def vec_sum(part, n):
-    rows, width = part.shape
-    return pl.pallas_call(
-        functools.partial(vec_sum_kernel, n),
-        in_specs=[pl.BlockSpec(memory_space=pltpu.VMEM)],
-        out_specs=pl.BlockSpec(memory_space=pltpu.VMEM),
-        out_shape=jax.ShapeDtypeStruct((rows, width), F32),
-        scratch_shapes=[pltpu.VMEM((n, rows, width), F32), pltpu.SemaphoreType.DMA((n,)), pltpu.SemaphoreType.DMA((n,))],
-        compiler_params=pltpu.CompilerParams(collective_id=1, has_side_effects=True),
-        name="vec_sum",
-    )(part)
-
-
 def layer_norm_fwd(token_rows, norm_gain, norm_bias):
     rows_f32 = token_rows.astype(jnp.float32)
     centered = rows_f32 - jnp.mean(rows_f32, axis=-1, keepdims=True)
@@ -226,46 +174,404 @@
     return act_value, act_slope
 
 
+MESH = pl.DeviceIdType.MESH
+
+
+def dot_nt(a, b):
+    return lax.dot_general(a, b, (((1,), (1,)), ((), ())), preferred_element_type=F32)
+
+
+def remote(src, dst, send_sem, recv_sem, dev):
+    return pltpu.make_async_remote_copy(src_ref=src, dst_ref=dst, send_sem=send_sem, recv_sem=recv_sem,
+                                        device_id={'tp': dev}, device_id_type=MESH)
+
+
+class Place:
+    def __init__(self, n, rows):
+        me = lax.axis_index('tp')
+        self.me, self.n, self.chips, self.half, self.rows = me, n, n // 2, rows // 2, rows
+        self.core, self.chip = lax.rem(me, 2), me // 2
+        self.partner = me + 1 - 2 * self.core
+        self.next = (lax.rem(me + 2, n), lax.rem(me + n - 2, n))
+
+    def origin(self, d, s):
+        return lax.rem(self.chip + (self.chips - s if d == 0 else s), self.chips)
+
+    def span(self, d, s, own):
+        core = self.core if own else 1 - self.core
+        start = (2 * self.origin(d, s) + core) * self.rows + d * self.half
+        return pl.ds(pl.multiple_of(start, self.half), self.half)
+
+    def greet(self):
+        barrier = pltpu.get_barrier_semaphore()
+        for dev in (self.next[0], self.next[1], self.partner):
+            pl.semaphore_signal(barrier, inc=1, device_id={'tp': dev}, device_id_type=MESH)
+        pl.semaphore_wait(barrier, 3)
+
+    def greet_all(self):
+        barrier = pltpu.get_barrier_semaphore()
+
+        def hello(r, _):
+            pl.semaphore_signal(barrier, inc=1, device_id={'tp': lax.rem(self.me + r, self.n)}, device_id_type=MESH)
+            return 0
+        lax.fori_loop(1, self.n, hello, 0)
+        pl.semaphore_wait(barrier, self.n - 1)
+
+
+class Gather:
+    def __init__(self, place, buf, send, recv, psend, precv):
+        self.p, self.buf, self.send, self.recv, self.psend, self.precv = place, buf, send, recv, psend, precv
+
+    def hop(self, d, s):
+        at = self.buf.at[self.p.span(d, s, True)]
+        return remote(at, at, self.send.at[d, s], self.recv.at[d, s], self.p.next[d])
+
+    def give(self, d, s):
+        at = self.buf.at[self.p.span(d, s, True)]
+        return remote(at, at, self.psend.at[d, s], self.precv.at[d, s], self.p.partner)
+
+    def pass_on(self, s, first=False):
+        for d in (0, 1):
+            if first:
+                self.hop(d, s).start()
+            else:
+                at = self.buf.at[self.p.span(d, s, True)]
+                remote(at, at, self.send.at[d, s - 1], self.recv.at[d, s - 1], self.p.next[d]).wait_recv()
+
+                @pl.when(s < self.p.chips - 1)
+                def _():
+                    self.hop(d, s).start()
+            self.give(d, s).start()
+
+    def arrive(self, d, s):
+        at = self.buf.at[self.p.span(d, s, False)]
+        remote(at, at, self.psend.at[d, s], self.precv.at[d, s], self.p.partner).wait_recv()
+
+    def load(self, d, s):
+        return jnp.concatenate([self.buf[self.p.span(d, s, True), :], self.buf[self.p.span(d, s, False), :]], axis=0)
+
+    def drain(self):
+        def one(s, _):
+            for d in (0, 1):
+                self.give(d, s).wait_send()
+
+                @pl.when(s < self.p.chips - 1)
+                def _():
+                    self.hop(d, s).wait_send()
+            return 0
+        lax.fori_loop(0, self.p.chips, one, 0)
+
+
+class Scatter:
+    def __init__(self, place, own, keep, out, inc, send, recv, pout, pinc, psend, precv):
+        self.p, self.own, self.keep, self.out, self.inc, self.send, self.recv = place, own, keep, out, inc, send, recv
+        self.pout, self.pinc, self.psend, self.precv = pout, pinc, psend, precv
+
+    def give(self, d, s):
+        return remote(self.pout.at[d, s], self.pinc.at[d, s], self.psend.at[d, s], self.precv.at[d, s], self.p.partner)
+
+    def hop(self, d, r):
+        return remote(self.out.at[d, r], self.inc.at[d, r], self.send.at[d, r], self.recv.at[d, r], self.p.next[d])
+
+    def put(self, d, s, part, first=False):
+        half = self.p.half
+        (self.keep if first else self.own)[d] = part[:half]
+        self.pout[d, s] = part[half:].astype(BF16)
+
+    def forward(self, d, s):
+        self.give(d, s).wait_recv()
+
+        @pl.when(s >= 2)
+        def _():
+            self.hop(d, s - 2).wait_recv()
+            self.own[d] += self.inc[d, s - 2].astype(F32)
+        self.out[d, s - 1] = (self.own[d] + self.pinc[d, s].astype(F32)).astype(BF16)
+
+    def final(self, d):
+        last = self.p.chips - 2
+        self.give(d, 0).wait_recv()
+        self.hop(d, last).wait_recv()
+        return self.keep[d] + self.pinc[d, 0].astype(F32) + self.inc[d, last].astype(F32)
+
+    def drain(self):
+        def one(s, _):
+            for d in (0, 1):
+                self.give(d, s).wait_send()
+
+                @pl.when(s < self.p.chips - 1)
+                def _():
+                    self.hop(d, s).wait_send()
+            return 0
+        lax.fori_loop(0, self.p.chips, one, 0)
+
+
+def gather_scratch(n, rows, width):
+    sems = [pltpu.SemaphoreType.DMA((2, n // 2))] * 4
+    return [pltpu.VMEM((n * rows, width), BF16)] + sems
+
+
+def scatter_scratch(n, rows, width):
+    chips, half = n // 2, rows // 2
+    sem = pltpu.SemaphoreType.DMA((2, chips))
+    wide = pltpu.VMEM((2, half, width), F32)
+    ring = pltpu.VMEM((2, chips - 1, half, width), BF16)
+    pair = pltpu.VMEM((2, chips, half, width), BF16)
+    return [wide, wide, ring, ring, sem, sem, pair, pair, sem, sem]
+
+
+def mlp_kernel(n, dout_hbm, dout, x_mid, z, gain, bias, w1, w2, dw1_out, dw2_out, db1_out, dmid_out, vec_out, *scratch):
+    gy_s, gh_s, rs_s, (w1_t, w2_t, dw1_t, load_sem) = scratch[:5], scratch[5:10], scratch[10:20], scratch[20:]
+    place = Place(n, x_mid.shape[0])
+    half = place.half
+    gy, gh, rs = Gather(place, *gy_s), Gather(place, *gh_s), Scatter(place, *rs_s)
+    mine = pl.ds(pl.multiple_of(place.me * place.rows, place.rows), place.rows)
+    load = pltpu.make_async_copy(dout_hbm, gy.buf.at[mine], load_sem)
+    load.start()
+    place.greet()
+    load.wait()
+    gy.pass_on(0, True)
+    gh.buf[mine, :] = layer_norm_fwd(x_mid[...], gain[...], bias[...])[2]
+    w1_t[...] = w1[...].T
+    w2_t[...] = w2[...].T
+    dw1_t[...] = jnp.zeros_like(dw1_t)
+    dw2_out[...] = jnp.zeros_like(dw2_out)
+    db1_out[...] = jnp.zeros_like(db1_out)
+    gh.pass_on(0, True)
+
+    def block(d, s, first):
+        gy.arrive(d, s)
+        dy = gy.load(d, s)
+        pre = jnp.concatenate([z[place.span(d, s, True), :], z[place.span(d, s, False), :]], axis=0).astype(F32)
+        act, slope = gelu_parts(pre)
+        dz = (dot(dy, w2_t[...]) * slope).astype(BF16)
+        rs.put(d, s, dot(dz, w1_t[...]), first)
+        if d == 1:
+            rs.give(0, s).start()
+        dw2_out[...] += dot(act.astype(BF16).T, dy)
+        db1_out[...] += jnp.sum(dz.astype(F32), axis=0, keepdims=True)
+        return dz
+
+    def late(d, s, dz):
+        gh.arrive(d, s)
+        dw1_t[...] += dot(dz.T, gh.load(d, s))
+
+    dz = [block(d, 0, True) for d in (0, 1)]
+    rs.give(1, 0).start()
+    for d in (0, 1):
+        late(d, 0, dz[d])
+
+    def step(s, _):
+        gy.pass_on(s)
+        dz = [block(d, s, False) for d in (0, 1)]
+        rs.give(1, s).start()
+        rs.forward(0, s)
+        rs.forward(1, s)
+        rs.hop(0, s - 1).start()
+        gh.pass_on(s)
+        rs.hop(1, s - 1).start()
+        for d in (0, 1):
+            late(d, s, dz[d])
+        return 0
+    lax.fori_loop(1, place.chips, step, 0)
+
+    vec = jnp.zeros((4, x_mid.shape[1]), F32)
+    for d in (0, 1):
+        rows = slice(d * half, (d + 1) * half)
+        x_hat, inv_std, _ = layer_norm_fwd(x_mid[rows, :], gain[...], bias[...])
+        grad = rs.final(d)
+        dy = dout[rows, :].astype(F32)
+        dmid = (dy + layer_norm_bwd(grad, x_hat, inv_std, gain[...])).astype(BF16)
+        dmid_out[rows, :] = dmid
+        vec += jnp.concatenate([jnp.sum(a, axis=0, keepdims=True) for a in (grad * x_hat, grad, dmid.astype(F32), dy)], axis=0)
+    vec_out[...] = vec
+    dw1_out[...] = dw1_t[...].T
+    for g in (gy, gh, rs):
+        g.drain()
+
+
+def comm_call(kernel, n, name, cid, args, out_shape, scratch, hbm=()):
+    vm = pl.BlockSpec(memory_space=pltpu.VMEM)
+    return pl.pallas_call(
+        functools.partial(kernel, n),
+        in_specs=[pl.BlockSpec(memory_space=pl.ANY) if i in hbm else vm for i in range(len(args))],
+        out_specs=[vm] * len(out_shape),
+        out_shape=[jax.ShapeDtypeStruct(*o) for o in out_shape],
+        scratch_shapes=scratch,
+        compiler_params=pltpu.CompilerParams(collective_id=cid, has_side_effects=True, vmem_limit_bytes=63 << 20),
+        name=name,
+    )(*args)
+
+
+def mlp_stage(n, dout, x_mid, z, gain, bias, w1, w2):
+    rows, width = dout.shape
+    units = z.shape[1]
+    scratch = gather_scratch(n, rows, width) * 2 + scatter_scratch(n, rows, width) + [
+        pltpu.VMEM((units, width), BF16), pltpu.VMEM((width, units), BF16), pltpu.VMEM((units, width), F32), pltpu.SemaphoreType.DMA]
+    return comm_call(mlp_kernel, n, "mlp_stage", 1, (dout, dout, x_mid, z, gain, bias, w1, w2),
+                     [((width, units), F32), ((units, width), F32), ((1, units), F32), ((rows, width), BF16), ((4, width), F32)], scratch, hbm=(0,))
+
+
+def mid_kernel(n, dmid_hbm, ctx_t, wo, dctx_out, dwo_out, *scratch):
+    g_s, load_sem = scratch[:5], scratch[5]
+    place = Place(n, dmid_hbm.shape[0])
+    g = Gather(place, *g_s)
+    mine = pl.ds(pl.multiple_of(place.me * place.rows, place.rows), place.rows)
+    load = pltpu.make_async_copy(dmid_hbm, g.buf.at[mine], load_sem)
+    load.start()
+    place.greet()
+    load.wait()
+    g.pass_on(0, True)
+    dwo_out[...] = jnp.zeros_like(dwo_out)
+
+    def block(d, s):
+        g.arrive(d, s)
+        dmid = g.load(d, s)
+        dctx = dot_nt(wo[...], dmid).astype(BF16)
+        cols = [place.span(d, s, own) for own in (True, False)]
+        dctx_out[:, cols[0]] = dctx[:, :place.half]
+        dctx_out[:, cols[1]] = dctx[:, place.half:]
+        dwo_out[...] += dot(jnp.concatenate([ctx_t[:, c] for c in cols], axis=1), dmid)
+
+    for d in (0, 1):
+        block(d, 0)
+
+    def step(s, _):
+        g.pass_on(s)
+        for d in (0, 1):
+            block(d, s)
+        return 0
+    lax.fori_loop(1, place.chips, step, 0)
+    g.drain()
+
+
+def mid_stage(n, dmid, ctx_t, wo):
+    rows, width = dmid.shape
+    dim, seq = ctx_t.shape
+    return comm_call(mid_kernel, n, "mid_stage", 2, (dmid, ctx_t, wo), [((dim, seq), BF16), ((dim, width), F32)],
+                     gather_scratch(n, rows, width) + [pltpu.SemaphoreType.DMA], hbm=(0,))
+
+
+class Spread:
+    def __init__(self, place, part, buf, send, recv):
+        self.p, self.part, self.buf, self.send, self.recv = place, part, buf, send, recv
+
+    def to(self, r):
+        me = self.p.me
+        return remote(self.part, self.buf.at[me], self.send.at[r], self.recv.at[me], lax.rem(me + r, self.p.n))
+
+    def start(self):
+        def one(r, _):
+            self.to(r).start()
+            return 0
+        lax.fori_loop(1, self.p.n, one, 0)
+        self.buf[pl.ds(self.p.me, 1)] = self.part[...][None]
+
+    def total(self):
+        def one(r, _):
+            src = lax.rem(self.p.me + self.p.n - r, self.p.n)
+            remote(self.part, self.buf.at[src], self.send.at[r], self.recv.at[src], src).wait_recv()
+            return 0
+        lax.fori_loop(1, self.p.n, one, 0)
+        return lax.fori_loop(1, self.p.n, lambda j, acc: acc + self.buf[j], self.buf[0])
+
+    def drain(self):
+        def one(r, _):
+            self.to(r).wait_send()
+            return 0
+        lax.fori_loop(1, self.p.n, one, 0)
+
+
+def qkv_kernel(n, dqkv_t, x_in, dmid, early, gain, bias, w_t, dx_out, dw_out, vec_out, *scratch):
+    gh_s, rs_s, (late_part, e_buf, e_send, e_recv, l_buf, l_send, l_recv) = scratch[:5], scratch[5:15], scratch[15:]
+    place = Place(n, x_in.shape[0])
+    half = place.half
+    gh, rs = Gather(place, *gh_s), Scatter(place, *rs_s)
+    first_rows, last_rows = Spread(place, early, e_buf, e_send, e_recv), Spread(place, late_part, l_buf, l_send, l_recv)
+    mine = pl.ds(pl.multiple_of(place.me * place.rows, place.rows), place.rows)
+    gh.buf[mine, :] = layer_norm_fwd(x_in[...], gain[...], bias[...])[2]
+    dw_out[...] = jnp.zeros_like(dw_out)
+    place.greet_all()
+
+    def cols(d, s):
+        return jnp.concatenate([dqkv_t[:, place.span(d, s, own)] for own in (True, False)], axis=1)
+
+    def block(d, s, first):
+        rs.put(d, s, dot(cols(d, s).T, w_t[...]), first)
+        if d == 1:
+            rs.give(0, s).start()
+
+    def late(d, s):
+        gh.arrive(d, s)
+        dw_out[...] += dot(cols(d, s), gh.load(d, s))
+
+    def scatter_step(s, hold):
+        block(0, s, False)
+        block(1, s, False)
+        rs.give(1, s).start()
+        rs.forward(0, s)
+        rs.forward(1, s)
+        rs.hop(0, s - 1).start()
+        if hold:
+            gh.pass_on(0, True)
+        else:
+            gh.pass_on(s - 1)
+        rs.hop(1, s - 1).start()
+        for d in (0, 1):
+            late(d, s - 1)
+
+    scatter_step(1, True)
+    first_rows.start()
+    block(0, 0, True)
+    block(1, 0, True)
+    rs.give(1, 0).start()
+
+    def step(s, _):
+        scatter_step(s, False)
+        return 0
+    lax.fori_loop(2, place.chips, step, 0)
+    gh.pass_on(place.chips - 1)
+
+    vec = jnp.zeros((2, x_in.shape[1]), F32)
+    for d in (0, 1):
+        rows = slice(d * half, (d + 1) * half)
+        x_hat, inv_std, _ = layer_norm_fwd(x_in[rows, :], gain[...], bias[...])
+        grad = rs.final(d)
+        dx_out[rows, :] = (dmid[rows, :].astype(F32) + layer_norm_bwd(grad, x_hat, inv_std, gain[...])).astype(BF16)
+        vec += jnp.concatenate([jnp.sum(grad * x_hat, axis=0, keepdims=True), jnp.sum(grad, axis=0, keepdims=True)], axis=0)
+    late_part[...] = vec
+    for d in (0, 1):
+        late(d, place.chips - 1)
+    last_rows.start()
+    vec_out[2:6, :] = first_rows.total()
+    vec_out[0:2, :] = last_rows.total()
+    for g in (gh, rs, first_rows, last_rows):
+        g.drain()
+
+
+def qkv_stage(n, dqkv_t, x_in, dmid, early, gain, bias, w_t):
+    rows, width = x_in.shape
+    sem = pltpu.SemaphoreType.DMA((n,))
+    scratch = gather_scratch(n, rows, width) + scatter_scratch(n, rows, width) + [
+        pltpu.VMEM((2, width), F32), pltpu.VMEM((n, 4, width), F32), sem, sem, pltpu.VMEM((n, 2, width), F32), sem, sem]
+    return comm_call(qkv_kernel, n, "qkv_stage", 3, (dqkv_t, x_in, dmid, early, gain, bias, w_t),
+                     [((rows, width), BF16), (w_t.shape, F32), ((6, width), F32)], scratch)
+
+
 def solution(mesh):
     def local_backward(x_in, x_mid, d_out, q_saved, k_saved, v_saved, z_saved, ln1_gain, ln1_bias, ln2_gain, ln2_bias, w_qkv, w_proj, w_fc1, w_fc2):
-        norm2_hat, norm2_rstd, h2_local = layer_norm_fwd(x_mid, ln2_gain, ln2_bias)
-        h2_full = lax.all_gather(h2_local, 'tp', axis=1, tiled=True)
-        dout_full = lax.all_gather(d_out, 'tp', axis=1, tiled=True)
-        act_value, act_slope = gelu_parts(z_saved.astype(jnp.float32))
-        grad_wfc2 = jnp.einsum('bsf,bsd->fd', act_value.astype(jnp.bfloat16), dout_full, preferred_element_type=jnp.float32)
-        grad_pre = (jnp.einsum('bsd,fd->bsf', dout_full, w_fc2, preferred_element_type=jnp.float32) * act_slope).astype(jnp.bfloat16)
-        grad_wfc1 = jnp.einsum('bsd,bsf->df', h2_full, grad_pre, preferred_element_type=jnp.float32)
-        grad_bfc1 = jnp.sum(grad_pre, axis=(0, 1), dtype=jnp.float32)
-        h2_partial = jnp.einsum('bsf,df->bsd', grad_pre, w_fc1, preferred_element_type=jnp.float32).astype(jnp.bfloat16)
-        grad_h2 = lax.psum_scatter(h2_partial, 'tp', scatter_dimension=1, tiled=True).astype(jnp.float32)
-        grad_mid = (d_out.astype(jnp.float32) + layer_norm_bwd(grad_h2, norm2_hat, norm2_rstd, ln2_gain)).astype(jnp.bfloat16)
-        mid_full = lax.all_gather(grad_mid, 'tp', axis=1, tiled=True)
-        norm1_hat, norm1_rstd, h1_local = layer_norm_fwd(x_in, ln1_gain, ln1_bias)
-        h1_full = lax.all_gather(h1_local, 'tp', axis=1, tiled=True)
+        n = mesh.shape['tp']
         dim = q_saved.shape[-1]
-        seq = q_saved.shape[1]
+        row = lambda a: a[None, :]
         q_t, k_t, v_t = (jnp.transpose(a[0, :, 0, :]) for a in (q_saved, k_saved, v_saved))
         lse, ctx_t, ctx_sum = attn_fwd(q_t, k_t, v_t)
-        dctx_t = jnp.einsum('ed,sd->es', w_proj[0], mid_full[0], preferred_element_type=jnp.float32).astype(jnp.bfloat16)
+        grad_wfc1, grad_wfc2, grad_bfc1, grad_mid, early = mlp_stage(n, d_out[0], x_mid[0], z_saved[0], row(ln2_gain), row(ln2_bias), w_fc1, w_fc2)
+        dctx_t, grad_wproj = mid_stage(n, grad_mid, ctx_t, w_proj[0])
         dqkv_t = attn_bwd(q_t, k_t, v_t, dctx_t, lse, ctx_sum)
-        grad_wproj = jnp.einsum('es,sd->ed', ctx_t, mid_full[0], preferred_element_type=jnp.float32)[None]
         w_qkv_t = jnp.transpose(w_qkv[:, :, 0, :], (0, 2, 1)).reshape(3 * dim, -1)
-        grad_w_t = jnp.einsum('es,sd->ed', dqkv_t, h1_full[0], preferred_element_type=jnp.float32)
+        grad_x, grad_w_t, grad_vecs = qkv_stage(n, dqkv_t, x_in[0], grad_mid, early, row(ln1_gain), row(ln1_bias), w_qkv_t)
         grad_wqkv = jnp.transpose(grad_w_t.reshape(3, dim, -1), (0, 2, 1))[:, :, None, :]
         grad_bqkv = jnp.sum(dqkv_t, axis=1, dtype=jnp.float32).reshape(3, 1, dim)
-        h1_partial = jnp.einsum('es,ed->sd', dqkv_t, w_qkv_t, preferred_element_type=jnp.float32).astype(jnp.bfloat16)[None]
-        grad_h1 = lax.psum_scatter(h1_partial, 'tp', scatter_dimension=1, tiled=True).astype(jnp.float32)
-        grad_x = (grad_mid.astype(jnp.float32) + layer_norm_bwd(grad_h1, norm1_hat, norm1_rstd, ln1_gain)).astype(jnp.bfloat16)
-        vec_partial = jnp.stack([
-            jnp.sum(grad_h1 * norm1_hat, axis=(0, 1)),
-            jnp.sum(grad_h1, axis=(0, 1)),
-            jnp.sum(grad_h2 * norm2_hat, axis=(0, 1)),
-            jnp.sum(grad_h2, axis=(0, 1)),
-            jnp.sum(grad_mid, axis=(0, 1), dtype=jnp.float32),
-            jnp.sum(d_out, axis=(0, 1), dtype=jnp.float32),
-        ])
-        grad_vecs = vec_sum(vec_partial, mesh.shape['tp'])
-        return grad_x, grad_wqkv, grad_bqkv, grad_wproj, grad_wfc1, grad_bfc1, grad_wfc2, grad_vecs
+        return grad_x[None], grad_wqkv, grad_bqkv, grad_wproj[None], grad_wfc1, grad_bfc1[0], grad_wfc2, grad_vecs
 
     tok_spec = P('dp', 'tp', None)
     head_spec = P('dp', None, 'tp', None)

time: 448 us -> 380 us (0.85)
  waiting for transfers between devices: 281 us -> 0 us
  Pallas kernels: 82.8 us -> 359 us
  matrix products: 53.3 us -> 0 us
  between operations: 14.3 us -> 0.74 us
  local copies, waits for them, and re-layouts: 5.43 us -> 18.9 us
  other arithmetic: 9.64 us -> 0.29 us
    pallas_call x1 -> x3, Pallas kernels: 25.1 us -> 302 us  [comm_call(): pl.pallas_call(functools.partial(kernel, n), in_specs=[pl.BlockSpec(memor...]
    all_gather x4 -> x0, waiting for transfers between devices: 157 us -> none  [the longest x1 59.1 us: local_backward(): dout_full = lax.all_gather(d_out, 'tp', axis=1, tiled=True)]
    reduce_scatter x2 -> x0, waiting for transfers between devices: 123 us -> none  [the longest x1 61.4 us: local_backward(): lax.psum_scatter(h2_partial, 'tp', scatter_dimension=1, tiled=True)]
    dot_general x8 -> x0, matrix products: 53.3 us -> none  [the longest x1 9.35 us: local_backward(): jnp.einsum('bsd,fd->bsf', dout_full, w_fc2, preferred_element_type=jnp.fl...]
    unnamed x43 -> x39, local copies, waits for them, and re-layouts: 4.13 us -> 18.3 us
    reduce_sum x7 -> x0, other arithmetic: 8.03 us -> none  [the longest x1 2.42 us: local_backward(): jnp.sum(grad_mid, axis=(0, 1), dtype=jnp.float32)]
  transfers between devices with their start and end apart: 6 -> 0, of which waited for: 6 -> 0; matrix products, arithmetic and copies ran while one was open for 6% -> 0% of each run, Pallas kernels for 11% -> 0%
where the time goes in v2:
time: 380 us; the launch traced here: 379 us
  Pallas kernels  359 us (94%)
  local copies, waits for them, and re-layouts  18.9 us (5%)
    pallas_call x3, Pallas kernels, comm_call(): pl.pallas_call(functools.partial(kernel, n), in_specs=[pl.BlockSpec(memor...  302 us
    pallas_call x1, Pallas kernels, attn_bwd(): pl.pallas_call(functools.partial(attn_bwd_kernel, blk), grid=(seq // blk,...  31.7 us
    pallas_call x1, Pallas kernels, attn_fwd(): pl.pallas_call(functools.partial(attn_fwd_kernel, blk), grid=(seq // blk,...  26.1 us
    unnamed x39, local copies, waits for them, and re-layouts  18.3 us

profile of v2, /device:TPU:21, one launch (start us, length us, event | category | flops | bytes accessed | tf_op | source)
XLA Modules:
  0.0 379.4 jit_solution(12605294889852949969)
XLA Ops:
  0.6 1.0 copy-done.2
  1.7 1.0 copy-done.4
  2.7 1.0 copy-done.6
  3.8 26.1 %attn_fwd.1 = (f32[8,4096]{1,0:T(8,128)S(1)}, bf16[64,4096]{1,0:T(8,128)(2,1)S(1)}, f32[64,4096]{1,0:T(8,128)S(1)}) custom-call(bf16[64,4096]{1,0:T(8,128)(2,1)S(1)} %bitcast.31, bf16[64,4096]{1,0:T(8,128)(2,1)S(1)} %bitcast.33, bf16[64,4096]{1,0:T(8,128)(2,1)S(1)} %bitcast.35), custom_call_target="tpu_custom_call" | custom-call | flops 12884901888 | bytes 2097152 | tf_op jit(solution)/shard_map/attn_fwd/pallas_call | solution.py:72
  29.8 0.8 copy-done.1
  30.6 1.0 copy-done.9
  31.6 135.3 %mlp_stage.1 = (f32[1024,256]{1,0:T(8,128)}, f32[256,1024]{1,0:T(8,128)}, f32[1,256]{1,0:T(1,128)}, bf16[256,1024]{1,0:T(8,128)(2,1)}, f32[4,1024]{1,0:T(4,128)}) custom-call(bf16[256,1024]{1,0:T(8,128)(2,1)} %bitcast.37, bf16[256,1024]{1,0:T(8,128)(2,1)} %bitcast.38, bf16[256,1024]{1,0:T(8,128)(2,1)} %bitcast.41, bf16[4096,256]{1,0:T(8,128)(2,1)} %bitcast.39, ...), custom_call_target="tpu_custom_call" | custom-call | tf_op jit(solution)/shard_map/mlp_stage/pallas_call | solution.py:394
  166.9 53.6 %mid_stage.1 = (bf16[64,4096]{1,0:T(8,128)(2,1)}, f32[64,1024]{1,0:T(8,128)}) custom-call(bf16[256,1024]{1,0:T(8,128)(2,1)} %get-tuple-element.21.dmid_hbm.dmid, bf16[64,4096]{1,0:T(8,128)(2,1)} %copy-done.1, bf16[64,1024]{1,0:T(8,128)(2,1)} %bitcast.46), custom_call_target="tpu_custom_call" | custom-call | tf_op jit(solution)/shard_map/mid_stage/pallas_call | solution.py:394
  220.5 1.0 copy-done.5
  221.5 1.0 copy-done.7
  222.5 1.0 copy-done.8
  223.6 1.2 copy-done.10
  224.8 31.7 %attn_bwd.1.dqkv_t = bf16[192,4096]{1,0:T(8,128)(2,1)S(1)} custom-call(bf16[64,4096]{1,0:T(8,128)(2,1)S(1)} %bitcast.32, bf16[64,4096]{1,0:T(8,128)(2,1)S(1)} %bitcast.34, bf16[64,4096]{1,0:T(8,128)(2,1)S(1)} %bitcast.36, bf16[64,4096]{1,0:T(8,128)(2,1)S(1)} %copy-done.8, f32[8,4096]{1,0:T(8,128)S(1)} %get-tuple-element.24.lse, f32[64,4096]{1,0:T(8,128)S(1)} %copy-done.10), custom_call_target="tpu_custom_call" | custom-call | flops 21474836480 | bytes 3670016 | tf_op jit(solution)/shard_map/attn_bwd/pallas_call | solution.py:142
  256.5 1.2 copy-done
  257.7 0.3 convert_reduce_fusion
  258.0 112.9 %qkv_stage.1 = (bf16[256,1024]{1,0:T(8,128)(2,1)}, f32[192,1024]{1,0:T(8,128)}, f32[6,1024]{1,0:T(8,128)}) custom-call(bf16[192,4096]{1,0:T(8,128)(2,1)} %copy-done, bf16[256,1024]{1,0:T(8,128)(2,1)} %bitcast.43, bf16[256,1024]{1,0:T(8,128)(2,1)} %get-tuple-element.21.dmid_hbm.dmid, f32[4,1024]{1,0:T(4,128)} %get-tuple-element.26.early, f32[1,1024]{1,0:T(1,128)} %bitcast.49, ...), custom_call_target="tpu_custom_call" | custom-call | tf_op jit(solution)/shard_map/qkv_stage/pallas_call | solution.py:394
  370.9 0.6 reshape.27
  371.5 1.9 copy.30
  373.4 2.2 copy.31
  375.6 0.7 copy.32
  376.3 1.0 copy.33
  377.3 0.6 copy.34
  377.8 1.0 copy.35
  378.8 0.6 copy.36
  (22 shorter events, 0.0 us)
Async XLA Ops:
  0.6 1.0 copy-start.2
  1.7 1.0 copy-start.4
  2.7 1.0 copy-start.6
  29.8 0.8 copy-start.1
  30.6 1.0 copy-start.9
  31.6 188.9 %copy-start.3 = (bf16[1,4096,1,64]{1,3,2,0:T(8,128)(2,1)S(1)}, bf16[1,4096,1,64]{1,3,2,0:T(8,128)(2,1)}, u32[]{:S(2)}) copy-start(bf16[1,4096,1,64]{1,3,2,0:T(8,128)(2,1)} %param.18) | copy-start | bytes 1572868
  220.4 1.0 copy-start.5
  221.5 1.0 copy-start.7
  222.5 1.0 copy-start.8
  223.6 1.2 copy-start.10
  256.5 1.2 copy-start
  258.0 117.6 %copy-start.13 = (f32[64,1024]{1,0:T(8,128)S(1)}, f32[64,1024]{1,0:T(8,128)}, u32[]{:S(2)}) copy-start(f32[64,1024]{1,0:T(8,128)} %get-tuple-element.29) | copy-start | bytes 786436
  370.9 5.4 %copy-start.12 = (f32[1024,256]{1,0:T(8,128)S(1)}, f32[1024,256]{1,0:T(8,128)}, u32[]{:S(2)}) copy-start(f32[1024,256]{1,0:T(8,128)} %get-tuple-element.46) | copy-start | bytes 3145732
  373.4 3.9 %copy-start.15 = (f32[1,256]{1,0:T(1,128)S(1)}, f32[1,256]{1,0:T(1,128)}, u32[]{:S(2)}) copy-start(f32[1,256]{1,0:T(1,128)} %get-tuple-element.31) | copy-start | bytes 3076
  373.4 4.4 %copy-start.11 = (f32[256,1024]{1,0:T(8,128)S(1)}, f32[256,1024]{1,0:T(8,128)}, u32[]{:S(2)}) copy-start(f32[256,1024]{1,0:T(8,128)} %get-tuple-element.48) | copy-start | bytes 3145732
  376.3 2.5 copy-start.14

commit v3 on v2

v3 whole, which is shorter than its diff:
```python
import functools
import jax, jax.numpy as jnp
from jax import lax
from jax.experimental import pallas as pl
from jax.experimental.pallas import tpu as pltpu
from jax.sharding import PartitionSpec as P

F32, BF16 = jnp.float32, jnp.bfloat16
LOG2E = 1.4426950408889634
LN_EPS = 1e-5
GELU_COEF = 0.044715
GELU_SCALE = 0.7978845608028654


def dot(a, b):
    return lax.dot_general(a, b, (((1,), (0,)), ((), ())), preferred_element_type=F32)


def layer_norm_fwd(token_rows, norm_gain, norm_bias):
    rows_f32 = token_rows.astype(jnp.float32)
    centered = rows_f32 - jnp.mean(rows_f32, axis=-1, keepdims=True)
    inv_std = lax.rsqrt(jnp.mean(centered * centered, axis=-1, keepdims=True) + LN_EPS)
    x_hat = centered * inv_std
    return x_hat, inv_std, (x_hat * norm_gain + norm_bias).astype(jnp.bfloat16)


def layer_norm_bwd(grad_norm, x_hat, inv_std, norm_gain):
    grad_hat = grad_norm * norm_gain
    centered_grad = grad_hat - jnp.mean(grad_hat, axis=-1, keepdims=True)
    return inv_std * (centered_grad - x_hat * jnp.mean(grad_hat * x_hat, axis=-1, keepdims=True))


def gelu_parts(pre_act):
    tanh_val = jnp.tanh(GELU_SCALE * (pre_act + GELU_COEF * pre_act * pre_act * pre_act))
    act_value = 0.5 * pre_act * (1.0 + tanh_val)
    act_slope = 0.5 * (1.0 + tanh_val) + 0.5 * pre_act * (1.0 - tanh_val * tanh_val) * GELU_SCALE * (1.0 + 3.0 * GELU_COEF * pre_act * pre_act)
    return act_value, act_slope


def attn_stats(step, blk, qT, kT, vT, k_rows, s_buf, lse_out, ctx_out, sum_out):
    dim, seq = kT.shape
    c = (dim ** -0.5) * LOG2E
    here = pl.ds(pl.multiple_of(step * blk, blk), blk)
    q = qT[:, here]
    k_rows[here, :] = kT[:, here].T

    def stats(i, carry, masked):
        m, l = carry
        rows = pl.ds(pl.multiple_of(i * blk, blk), blk)
        s = dot(k_rows[rows, :], q) * c
        if masked:
            r = lax.broadcasted_iota(jnp.int32, (blk, blk), 0)
            col = lax.broadcasted_iota(jnp.int32, (blk, blk), 1)
            s = jnp.where(r <= col, s, -1e30)
        s_buf[rows, :] = s
        new = jnp.maximum(m, jnp.max(s, axis=0, keepdims=True))
        l = l * jnp.exp2(m - new) + jnp.sum(jnp.exp2(s - new), axis=0, keepdims=True)
        return new, l

    init = (jnp.full((1, blk), -1e30, F32), jnp.zeros((1, blk), F32))
    carry = lax.fori_loop(0, step, functools.partial(stats, masked=False), init)
    m, l = stats(step, carry, True)
    lse = m + jnp.log2(l)

    def apply(i, carry):
        low_sum, res_sum = carry
        rows = pl.ds(pl.multiple_of(i * blk, blk), blk)
        p = jnp.exp2(s_buf[rows, :] - lse)
        low = p.astype(BF16)
        res = (p - low.astype(F32)).astype(BF16)
        v = vT[:, rows]
        return low_sum + dot(v, low), res_sum + dot(v, res)

    zero = jnp.zeros((dim, blk), F32)
    low_sum, res_sum = lax.fori_loop(0, step + 1, apply, (zero, zero))
    ctx_out[:, here] = low_sum.astype(BF16)
    sum_out[:, here] = low_sum + res_sum
    lse_out[:, here] = jnp.broadcast_to(lse, (8, blk))


def attn_grads(blk, qT, kT, vT, dctxT, lse, ctxsum, out, k_rows, dk_acc, dv_acc, service):
    dim, seq = kT.shape
    scale = dim ** -0.5
    c = scale * LOG2E

    def turn(i, _):
        cols = pl.ds(pl.multiple_of(i * blk, blk), blk)
        k_rows[cols, :] = kT[:, cols].T
        dk_acc[:, cols] = jnp.zeros((dim, blk), F32)
        dv_acc[:, cols] = jnp.zeros((dim, blk), F32)
        return 0
    lax.fori_loop(0, seq // blk, turn, 0)

    def queries(step, _):
        here = pl.ds(pl.multiple_of(step * blk, blk), blk)
        qt = qT[:, here]
        dct = dctxT[:, here]
        q = qt.T
        dc = dct.T
        delta_row = jnp.sum(dct.astype(F32) * ctxsum[:, here], axis=0, keepdims=True)
        lse_col = jnp.broadcast_to(lse[0:1, here], (128, blk)).T[:, :1]
        delta_col = jnp.broadcast_to(delta_row, (128, blk)).T[:, :1]
        base = step * (step + 1) // 2

        def block(i, dq, masked):
            service(base + i)
            cols = pl.ds(pl.multiple_of(i * blk, blk), blk)
            s = dot(q, kT[:, cols]) * c
            dp = dot(dc, vT[:, cols])
            p = jnp.exp2(s - lse_col)
            if masked:
                r = lax.broadcasted_iota(jnp.int32, (blk, blk), 0)
                col = lax.broadcasted_iota(jnp.int32, (blk, blk), 1)
                p = jnp.where(r >= col, p, 0.0)
            ds = (p * (dp - delta_col)).astype(BF16)
            dv_acc[:, cols] += dot(dct, p.astype(BF16))
            dk_acc[:, cols] += dot(qt, ds)
            return dq + dot(ds, k_rows[cols, :])

        dq = lax.fori_loop(0, step, functools.partial(block, masked=False), jnp.zeros((blk, dim), F32))
        dq = block(step, dq, True)
        out[0:dim, here] = (dq * scale).T.astype(BF16)
        return 0
    lax.fori_loop(0, seq // blk, queries, 0)

    def put(i, _):
        cols = pl.ds(pl.multiple_of(i * blk, blk), blk)
        out[dim:2 * dim, cols] = (dk_acc[:, cols] * scale).astype(BF16)
        out[2 * dim:3 * dim, cols] = dv_acc[:, cols].astype(BF16)
        return 0
    lax.fori_loop(0, seq // blk, put, 0)


MESH = pl.DeviceIdType.MESH
SUBS = 2


def dot_nt(a, b):
    return lax.dot_general(a, b, (((1,), (1,)), ((), ())), preferred_element_type=F32)


def remote(src, dst, send_sem, recv_sem, dev):
    return pltpu.make_async_remote_copy(src_ref=src, dst_ref=dst, send_sem=send_sem, recv_sem=recv_sem,
                                        device_id={'tp': dev}, device_id_type=MESH)


class Place:
    def __init__(self, n, rows):
        me = lax.axis_index('tp')
        self.me, self.n, self.chips, self.half, self.rows = me, n, n // 2, rows // 2, rows
        self.core, self.chip = lax.rem(me, 2), me // 2
        self.partner = me + 1 - 2 * self.core
        self.next = (lax.rem(me + 2, n), lax.rem(me + n - 2, n))
        self.sub = self.half // SUBS

    def origin(self, d, s):
        return lax.rem(self.chip + (self.chips - s if d == 0 else s), self.chips)

    def span(self, d, s, own):
        core = self.core if own else 1 - self.core
        start = (2 * self.origin(d, s) + core) * self.rows + d * self.half
        return pl.ds(pl.multiple_of(start, self.half), self.half)

    def part(self, d, s, own, sub):
        core = self.core if own else 1 - self.core
        start = (2 * self.origin(d, s) + core) * self.rows + d * self.half + sub * self.sub
        return pl.ds(pl.multiple_of(start, self.sub), self.sub)

    def greet(self):
        barrier = pltpu.get_barrier_semaphore()
        for dev in (self.next[0], self.next[1], self.partner):
            pl.semaphore_signal(barrier, inc=1, device_id={'tp': dev}, device_id_type=MESH)
        pl.semaphore_wait(barrier, 3)

    def greet_all(self):
        barrier = pltpu.get_barrier_semaphore()

        def hello(r, _):
            pl.semaphore_signal(barrier, inc=1, device_id={'tp': lax.rem(self.me + r, self.n)}, device_id_type=MESH)
            return 0
        lax.fori_loop(1, self.n, hello, 0)
        pl.semaphore_wait(barrier, self.n - 1)


class Gather:
    def __init__(self, place, buf, send, recv, psend, precv):
        self.p, self.buf, self.send, self.recv, self.psend, self.precv = place, buf, send, recv, psend, precv

    def hop(self, d, s, sub):
        at = self.buf.at[self.p.part(d, s, True, sub)]
        return remote(at, at, self.send.at[d, s, sub], self.recv.at[d, s, sub], self.p.next[d])

    def give(self, d, s, sub):
        at = self.buf.at[self.p.part(d, s, True, sub)]
        return remote(at, at, self.psend.at[d, s, sub], self.precv.at[d, s, sub], self.p.partner)

    def first(self):
        for sub in range(SUBS):
            for d in (0, 1):
                self.hop(d, 0, sub).start()
        for sub in range(SUBS):
            for d in (0, 1):
                self.give(d, 0, sub).start()

    def pass_one(self, s, sub):
        for d in (0, 1):
            at = self.buf.at[self.p.part(d, s, True, sub)]
            remote(at, at, self.send.at[d, s - 1, sub], self.recv.at[d, s - 1, sub], self.p.next[d]).wait_recv()

            @pl.when(s < self.p.chips - 1)
            def _():
                self.hop(d, s, sub).start()
            self.give(d, s, sub).start()

    def pass_on(self, s):
        for sub in range(SUBS):
            self.pass_one(s, sub)

    def arrive(self, d, s):
        for sub in range(SUBS):
            at = self.buf.at[self.p.part(d, s, False, sub)]
            remote(at, at, self.psend.at[d, s, sub], self.precv.at[d, s, sub], self.p.partner).wait_recv()

    def load(self, d, s):
        return jnp.concatenate([self.buf[self.p.span(d, s, True), :], self.buf[self.p.span(d, s, False), :]], axis=0)

    def drain(self):
        def one(s, _):
            for d in (0, 1):
                for sub in range(SUBS):
                    self.give(d, s, sub).wait_send()

                    @pl.when(s < self.p.chips - 1)
                    def _():
                        self.hop(d, s, sub).wait_send()
            return 0
        lax.fori_loop(0, self.p.chips, one, 0)


class Scatter:
    def __init__(self, place, own, keep, out, inc, send, recv, pout, pinc, psend, precv):
        self.p, self.own, self.keep, self.out, self.inc, self.send, self.recv = place, own, keep, out, inc, send, recv
        self.pout, self.pinc, self.psend, self.precv = pout, pinc, psend, precv

    def give(self, d, s):
        return remote(self.pout.at[d, s], self.pinc.at[d, s], self.psend.at[d, s], self.precv.at[d, s], self.p.partner)

    def hop(self, d, r, sub):
        rows = slice(sub * self.p.sub, (sub + 1) * self.p.sub)
        return remote(self.out.at[d, r, rows], self.inc.at[d, r, rows], self.send.at[d, r, sub], self.recv.at[d, r, sub], self.p.next[d])

    def put(self, d, s, part, first=False):
        half = self.p.half
        (self.keep if first else self.own)[d] = part[:half]
        self.pout[d, s] = part[half:].astype(BF16)

    def join(self, d, s):
        self.give(d, s).wait_recv()
        self.own[d] += self.pinc[d, s].astype(F32)

    def forward(self, d, s, sub):
        rows = slice(sub * self.p.sub, (sub + 1) * self.p.sub)

        @pl.when(s >= 2)
        def _():
            self.hop(d, s - 2, sub).wait_recv()
            self.out[d, s - 1, rows] = (self.own[d, rows] + self.inc[d, s - 2, rows].astype(F32)).astype(BF16)

        @pl.when(s < 2)
        def _():
            self.out[d, s - 1, rows] = self.own[d, rows].astype(BF16)

    def pass_on(self, s):
        for d in (0, 1):
            self.join(d, s)
        before = None
        for sub in range(SUBS):
            for d in (0, 1):
                self.forward(d, s, sub)
                if before is not None:
                    self.hop(*before).start()
                before = (d, s - 1, sub)
        return self.hop(*before)

    def final(self, d, store):
        last = self.p.chips - 2
        self.give(d, 0).wait_recv()
        for sub in range(SUBS):
            self.hop(d, last, sub).wait_recv()
        return store[d] + self.pinc[d, 0].astype(F32) + self.inc[d, last].astype(F32)

    def drain(self):
        def one(s, _):
            for d in (0, 1):
                self.give(d, s).wait_send()
                for sub in range(SUBS):
                    @pl.when(s < self.p.chips - 1)
                    def _():
                        self.hop(d, s, sub).wait_send()
            return 0
        lax.fori_loop(0, self.p.chips, one, 0)


def gather_scratch(n, rows, width):
    sems = [pltpu.SemaphoreType.DMA((2, n // 2, SUBS))] * 4
    return [pltpu.VMEM((n * rows, width), BF16)] + sems


def scatter_scratch(n, rows, width):
    chips, half = n // 2, rows // 2
    sem = pltpu.SemaphoreType.DMA((2, chips))
    fine = pltpu.SemaphoreType.DMA((2, chips, SUBS))
    wide = pltpu.VMEM((2, half, width), F32)
    ring = pltpu.VMEM((2, chips - 1, half, width), BF16)
    pair = pltpu.VMEM((2, chips, half, width), BF16)
    return [wide, wide, ring, ring, fine, fine, pair, pair, sem, sem]


def mlp_kernel(n, dout_hbm, dout, x_mid, z, gain, bias, w1, w2, qT, kT, vT,
               dw1_out, dw2_out, db1_out, dmid_out, vec_out, lse_out, ctx_out, sum_out, *scratch):
    gy_s, gh_s, rs_s, (w1_t, w2_t, dw1_t, load_sem, k_rows, s_buf) = scratch[:5], scratch[5:10], scratch[10:20], scratch[20:]
    place = Place(n, x_mid.shape[0])
    half = place.half
    blk = kT.shape[1] // place.chips
    gy, gh, rs = Gather(place, *gy_s), Gather(place, *gh_s), Scatter(place, *rs_s)
    mine = pl.ds(pl.multiple_of(place.me * place.rows, place.rows), place.rows)
    load = pltpu.make_async_copy(dout_hbm, gy.buf.at[mine], load_sem)
    load.start()
    place.greet()
    load.wait()
    gy.first()
    gh.buf[mine, :] = layer_norm_fwd(x_mid[...], gain[...], bias[...])[2]
    w1_t[...] = w1[...].T
    w2_t[...] = w2[...].T
    dw1_t[...] = jnp.zeros_like(dw1_t)
    dw2_out[...] = jnp.zeros_like(dw2_out)
    db1_out[...] = jnp.zeros_like(db1_out)
    gh.first()

    def block(d, s, first):
        gy.arrive(d, s)
        dy = gy.load(d, s)
        pre = jnp.concatenate([z[place.span(d, s, True), :], z[place.span(d, s, False), :]], axis=0).astype(F32)
        act, slope = gelu_parts(pre)
        dz = (dot(dy, w2_t[...]) * slope).astype(BF16)
        rs.put(d, s, dot(dz, w1_t[...]), first)
        if d == 1:
            rs.give(0, s).start()
        dw2_out[...] += dot(act.astype(BF16).T, dy)
        db1_out[...] += jnp.sum(dz.astype(F32), axis=0, keepdims=True)
        return dz

    def late(d, s, dz):
        gh.arrive(d, s)
        dw1_t[...] += dot(dz.T, gh.load(d, s))

    def attend(s):
        attn_stats(s, blk, qT, kT, vT, k_rows, s_buf, lse_out, ctx_out, sum_out)

    dz = [block(d, 0, True) for d in (0, 1)]
    rs.give(1, 0).start()
    for d in (0, 1):
        late(d, 0, dz[d])
    attend(0)

    def step(s, _):
        gy.pass_on(s)
        dz = [block(d, s, False) for d in (0, 1)]
        rs.give(1, s).start()
        tail = rs.pass_on(s)
        gh.pass_on(s)
        tail.start()
        for d in (0, 1):
            late(d, s, dz[d])
        attend(s)
        return 0
    lax.fori_loop(1, place.chips, step, 0)
    dw1_out[...] = dw1_t[...].T

    vec = jnp.zeros((4, x_mid.shape[1]), F32)
    for d in (0, 1):
        rows = slice(d * half, (d + 1) * half)
        x_hat, inv_std, _ = layer_norm_fwd(x_mid[rows, :], gain[...], bias[...])
        grad = rs.final(d, rs.keep)
        dy = dout[rows, :].astype(F32)
        dmid = (dy + layer_norm_bwd(grad, x_hat, inv_std, gain[...])).astype(BF16)
        dmid_out[rows, :] = dmid
        vec += jnp.concatenate([jnp.sum(a, axis=0, keepdims=True) for a in (grad * x_hat, grad, dmid.astype(F32), dy)], axis=0)
    vec_out[...] = vec
    for g in (gy, gh, rs):
        g.drain()


def comm_call(kernel, n, name, cid, args, out_shape, scratch, limit, hbm=()):
    vm = pl.BlockSpec(memory_space=pltpu.VMEM)
    return pl.pallas_call(
        functools.partial(kernel, n),
        in_specs=[pl.BlockSpec(memory_space=pl.ANY) if i in hbm else vm for i in range(len(args))],
        out_specs=[vm] * len(out_shape),
        out_shape=[jax.ShapeDtypeStruct(*o) for o in out_shape],
        scratch_shapes=scratch,
        compiler_params=pltpu.CompilerParams(collective_id=cid, has_side_effects=True, vmem_limit_bytes=limit << 20),
        name=name,
    )(*args)


def mlp_stage(n, dout, x_mid, z, gain, bias, w1, w2, q_t, k_t, v_t):
    rows, width = dout.shape
    units = z.shape[1]
    dim, seq = q_t.shape
    scratch = gather_scratch(n, rows, width) * 2 + scatter_scratch(n, rows, width) + [
        pltpu.VMEM((units, width), BF16), pltpu.VMEM((width, units), BF16), pltpu.VMEM((units, width), F32), pltpu.SemaphoreType.DMA,
        pltpu.VMEM((seq, dim), BF16), pltpu.VMEM((seq, 2 * seq // n), F32)]
    return comm_call(mlp_kernel, n, "mlp_stage", 1, (dout, dout, x_mid, z, gain, bias, w1, w2, q_t, k_t, v_t),
                     [((width, units), F32), ((units, width), F32), ((1, units), F32), ((rows, width), BF16), ((4, width), F32),
                      ((8, seq), F32), ((dim, seq), BF16), ((dim, seq), F32)], scratch, 63, hbm=(0,))


class Spread:
    def __init__(self, place, part, buf, send, recv):
        self.p, self.part, self.buf, self.send, self.recv = place, part, buf, send, recv

    def to(self, r):
        me = self.p.me
        return remote(self.part, self.buf.at[me], self.send.at[r], self.recv.at[me], lax.rem(me + r, self.p.n))

    def start(self):
        def one(r, _):
            self.to(r).start()
            return 0
        lax.fori_loop(1, self.p.n, one, 0)
        self.buf[pl.ds(self.p.me, 1)] = self.part[...][None]

    def total(self):
        def one(r, _):
            src = lax.rem(self.p.me + self.p.n - r, self.p.n)
            remote(self.part, self.buf.at[src], self.send.at[r], self.recv.at[src], src).wait_recv()
            return 0
        lax.fori_loop(1, self.p.n, one, 0)
        return lax.fori_loop(1, self.p.n, lambda j, acc: acc + self.buf[j], self.buf[0])

    def drain(self):
        def one(r, _):
            self.to(r).wait_send()
            return 0
        lax.fori_loop(1, self.p.n, one, 0)


def attn_kernel(n, dmid_hbm, dmid, ctx_t, ctx_sum, lse, qT, kT, vT, wo, x_in, early, gain, bias, w_t,
                dwo_out, dx_out, dw_out, db_out, vec_out, *scratch):
    g_s, gh_s, rs_s = scratch[:5], scratch[5:10], scratch[10:20]
    load_sem, dctx, dqkv_t, k_rows, dk_acc, dv_acc, late_part, e_buf, e_send, e_recv, l_buf, l_send, l_recv = scratch[20:]
    place = Place(n, x_in.shape[0])
    half, chips = place.half, place.chips
    seq = kT.shape[1]
    blk = seq // chips
    g, gh, rs = Gather(place, *g_s), Gather(place, *gh_s), Scatter(place, *rs_s)
    first_rows, last_rows = Spread(place, early, e_buf, e_send, e_recv), Spread(place, late_part, l_buf, l_send, l_recv)
    mine = pl.ds(pl.multiple_of(place.me * place.rows, place.rows), place.rows)
    load = pltpu.make_async_copy(dmid_hbm, g.buf.at[mine], load_sem)
    load.start()
    place.greet_all()
    load.wait()
    g.first()
    gh.buf[mine, :] = layer_norm_fwd(x_in[...], gain[...], bias[...])[2]
    dwo_out[...] = jnp.zeros_like(dwo_out)
    dw_out[...] = jnp.zeros_like(dw_out)
    db_out[...] = jnp.zeros_like(db_out)

    def project(d, s):
        g.arrive(d, s)
        rows = g.load(d, s)
        both = dot_nt(wo[...], rows).astype(BF16)
        cols = [place.span(d, s, own) for own in (True, False)]
        dctx[:, cols[0]] = both[:, :half]
        dctx[:, cols[1]] = both[:, half:]
        dwo_out[...] += dot(jnp.concatenate([ctx_t[:, c] for c in cols], axis=1), rows)

    for d in (0, 1):
        project(d, 0)

    def mid_step(s, _):
        g.pass_on(s)
        for d in (0, 1):
            project(d, s)
        return 0
    lax.fori_loop(1, chips - 1, mid_step, 0)
    g.pass_on(chips - 1)
    gh.first()
    first_rows.start()
    for d in (0, 1):
        project(d, chips - 1)

    stride = 3
    blocks = chips * (chips + 1) // 2
    done = (blocks + stride - 1) // stride
    events = SUBS * (chips - 1)

    def service(e):
        ev = e // stride

        @pl.when((lax.rem(e, stride) == 0) & (ev < events))
        def _():
            gh.pass_one(1 + ev // SUBS, lax.rem(ev, SUBS))

    attn_grads(blk, qT, kT, vT, dctx, lse, ctx_sum, dqkv_t, k_rows, dk_acc, dv_acc, service)

    def cols_of(d, s):
        return jnp.concatenate([dqkv_t[:, place.span(d, s, own)] for own in (True, False)], axis=1)

    def block(s):
        for d in (0, 1):
            rs.put(d, s, dot(cols_of(d, s).T, w_t[...]))
            if d == 1:
                rs.give(0, s).start()

    def late(d, s):
        gh.arrive(d, s)
        cols = cols_of(d, s)
        dw_out[...] += dot(cols, gh.load(d, s))
        db_out[...] += jnp.sum(cols.astype(F32), axis=1, keepdims=True)

    block(1)
    rs.give(1, 1).start()

    def step(s, _):
        tail = rs.pass_on(s)
        following = lax.rem(s + 1, chips)
        block(following)
        tail.start()
        rs.give(1, following).start()
        ev = done + s - 2

        @pl.when((s >= 2) & (ev < events))
        def _():
            gh.pass_one(1 + ev // SUBS, lax.rem(ev, SUBS))
        for d in (0, 1):
            late(d, s - 1)
        return 0
    lax.fori_loop(1, chips, step, 0)

    vec = jnp.zeros((2, x_in.shape[1]), F32)
    for d in (0, 1):
        rows = slice(d * half, (d + 1) * half)
        x_hat, inv_std, _ = layer_norm_fwd(x_in[rows, :], gain[...], bias[...])
        grad = rs.final(d, rs.own)
        dx_out[rows, :] = (dmid[rows, :].astype(F32) + layer_norm_bwd(grad, x_hat, inv_std, gain[...])).astype(BF16)
        vec += jnp.concatenate([jnp.sum(grad * x_hat, axis=0, keepdims=True), jnp.sum(grad, axis=0, keepdims=True)], axis=0)
    late_part[...] = vec
    vec_out[2:6, :] = first_rows.total()
    last_rows.start()
    for d in (0, 1):
        late(d, chips - 1)
    vec_out[0:2, :] = last_rows.total()
    for one in (g, gh, rs, first_rows, last_rows):
        one.drain()


def attn_stage(n, dmid, ctx_t, ctx_sum, lse, q_t, k_t, v_t, wo, x_in, early, gain, bias, w_t):
    rows, width = x_in.shape
    dim, seq = q_t.shape
    sem = pltpu.SemaphoreType.DMA((n,))
    acc = pltpu.VMEM((dim, seq), F32)
    scratch = gather_scratch(n, rows, width) * 2 + scatter_scratch(n, rows, width) + [
        pltpu.SemaphoreType.DMA, pltpu.VMEM((dim, seq), BF16), pltpu.VMEM((3 * dim, seq), BF16), pltpu.VMEM((seq, dim), BF16), acc, acc,
        pltpu.VMEM((2, width), F32), pltpu.VMEM((n, 4, width), F32), sem, sem, pltpu.VMEM((n, 2, width), F32), sem, sem]
    return comm_call(attn_kernel, n, "attn_stage", 2,
                     (dmid, dmid, ctx_t, ctx_sum, lse, q_t, k_t, v_t, wo, x_in, early, gain, bias, w_t),
                     [((dim, width), F32), ((rows, width), BF16), (w_t.shape, F32), ((3 * dim, 1), F32), ((6, width), F32)], scratch, 63, hbm=(0,))


def solution(mesh):
    def local_backward(x_in, x_mid, d_out, q_saved, k_saved, v_saved, z_saved, ln1_gain, ln1_bias, ln2_gain, ln2_bias, w_qkv, w_proj, w_fc1, w_fc2):
        n = mesh.shape['tp']
        dim = q_saved.shape[-1]
        row = lambda a: a[None, :]
        q_t, k_t, v_t = (jnp.transpose(a[0, :, 0, :]) for a in (q_saved, k_saved, v_saved))
        grad_wfc1, grad_wfc2, grad_bfc1, grad_mid, early, lse, ctx_t, ctx_sum = mlp_stage(
            n, d_out[0], x_mid[0], z_saved[0], row(ln2_gain), row(ln2_bias), w_fc1, w_fc2, q_t, k_t, v_t)
        w_qkv_t = jnp.transpose(w_qkv[:, :, 0, :], (0, 2, 1)).reshape(3 * dim, -1)
        grad_wproj, grad_x, grad_w_t, grad_b, grad_vecs = attn_stage(
            n, grad_mid, ctx_t, ctx_sum, lse, q_t, k_t, v_t, w_proj[0], x_in[0], early, row(ln1_gain), row(ln1_bias), w_qkv_t)
        grad_wqkv = jnp.transpose(grad_w_t.reshape(3, dim, -1), (0, 2, 1))[:, :, None, :]
        return grad_x[None], grad_wqkv, grad_b.reshape(3, 1, dim), grad_wproj[None], grad_wfc1, grad_bfc1[0], grad_wfc2, grad_vecs

    tok_spec = P('dp', 'tp', None)
    head_spec = P('dp', None, 'tp', None)
    in_specs = (tok_spec, tok_spec, tok_spec, head_spec, head_spec, head_spec, P('dp', None, 'tp'),
                P(None), P(None), P(None), P(None),
                P(None, None, 'tp', None), P('tp', None, None), P(None, 'tp'), P('tp', None))
    out_specs = (tok_spec, P('dp', None, 'tp', None), P('dp', 'tp', None), P(('dp', 'tp'), None, None),
                 P('dp', 'tp'), P(('dp', 'tp')), P(('dp', 'tp'), None), P('dp', None))
    return jax.shard_map(local_backward, mesh=mesh, in_specs=in_specs, out_specs=out_specs, check_vma=False)
```

time: 380 us -> 305 us (0.80)
  Pallas kernels: 359 us -> 295 us
  local copies, waits for them, and re-layouts: 18.9 us -> 8.54 us
    pallas_call x2 -> x0, Pallas kernels: 57.7 us -> none  [the longest x1 31.7 us: attn_bwd(): pl.pallas_call(functools.partial(attn_bwd_kernel, blk), grid=(seq // blk,...]
    unnamed x39 -> x17, local copies, waits for them, and re-layouts: 18.3 us -> 7.88 us
    pallas_call x3 -> x2, Pallas kernels: 302 us -> 295 us  [comm_call(): pl.pallas_call(functools.partial(kernel, n), in_specs=[pl.BlockSpec(memor...]
where the time goes in v3:
time: 305 us
  Pallas kernels  295 us (97%)
  local copies, waits for them, and re-layouts  8.54 us (3%)
    pallas_call x2, Pallas kernels, comm_call(): pl.pallas_call(functools.partial(kernel, n), in_specs=[pl.BlockSpec(memor...  295 us
    unnamed x17, local copies, waits for them, and re-layouts  7.88 us

profile of v3, /device:TPU:21, one launch (start us, length us, event | category | flops | bytes accessed | tf_op | source)
XLA Modules:
  0.0 305.2 jit_solution(713048403890253)
XLA Ops:
  0.6 140.9 %mlp_stage.1 = (f32[1024,256]{1,0:T(8,128)}, f32[256,1024]{1,0:T(8,128)}, f32[1,256]{1,0:T(1,128)}, bf16[256,1024]{1,0:T(8,128)(2,1)}, f32[4,1024]{1,0:T(4,128)}...) custom-call(bf16[256,1024]{1,0:T(8,128)(2,1)} %bitcast.31, bf16[256,1024]{1,0:T(8,128)(2,1)} %bitcast.32, ...), custom_call_target="tpu_custom_call" | custom-call | tf_op jit(solution)/shard_map/mlp_stage/pallas_call | solution.py:396
  141.5 154.0 %attn_stage.1 = (f32[64,1024]{1,0:T(8,128)}, bf16[256,1024]{1,0:T(8,128)(2,1)}, f32[192,1024]{1,0:T(8,128)}, f32[192,1]{1,0:T(8,128)}, f32[6,1024]{1,0:T(8,128)}) custom-call(bf16[256,1024]{1,0:T(8,128)(2,1)} %get-tuple-element.21.dmid_hbm.dmid, bf16[256,1024]{1,0:T(8,128)(2,1)} %get-tuple-element.21.dmid_hbm.dmid, ...), custom_call_target="tpu_custom_call" | custom-call | tf_op jit(solution)/shard_map/attn_stage/pallas_call | solution.py:396
  295.5 0.0 copy-start.2
  295.5 0.0 copy-start.1
  295.5 1.1 reduce
  296.6 0.7 reshape.28
  297.3 1.9 copy.32
  299.2 0.0 copy-start.4
  299.2 0.0 copy-start
  299.2 2.2 copy.33
  301.3 0.0 copy-done.2
  301.3 0.7 copy.34
  302.0 0.0 copy-done.1
  302.0 0.0 copy-start.3
  302.0 1.0 copy.35
  303.0 0.0 copy-done.4
  303.0 0.6 copy.36
  303.6 0.0 copy-done
  303.6 1.0 copy.37
  304.6 0.0 copy-done.3
  304.6 0.6 copy.38
Async XLA Ops:
  295.5 5.8 %copy-start.2 = (f32[64,1024]{1,0:T(8,128)S(1)}, f32[64,1024]{1,0:T(8,128)}, u32[]{:S(2)}) copy-start(f32[64,1024]{1,0:T(8,128)} %get-tuple-element.29) | copy-start | bytes 786436
  295.5 6.5 %copy-start.1 = (f32[1024,256]{1,0:T(8,128)S(1)}, f32[1024,256]{1,0:T(8,128)}, u32[]{:S(2)}) copy-start(f32[1024,256]{1,0:T(8,128)} %get-tuple-element.62) | copy-start | bytes 3145732
  299.2 3.9 %copy-start.4 = (f32[1,256]{1,0:T(1,128)S(1)}, f32[1,256]{1,0:T(1,128)}, u32[]{:S(2)}) copy-start(f32[1,256]{1,0:T(1,128)} %get-tuple-element.31) | copy-start | bytes 3076
  299.2 4.4 %copy-start = (f32[256,1024]{1,0:T(8,128)S(1)}, f32[256,1024]{1,0:T(8,128)}, u32[]{:S(2)}) copy-start(f32[256,1024]{1,0:T(8,128)} %get-tuple-element.64) | copy-start | bytes 3145732
  302.0 2.5 copy-start.3

commit v4 on v3

--- a/solution.py
+++ b/solution.py
@@ -37,22 +37,25 @@
     return act_value, act_slope
 
 
-def attn_stats(step, blk, qT, kT, vT, k_rows, s_buf, lse_out, ctx_out, sum_out):
+def attn_stats(step, blk, qT, kT, vT, k_rows, lse_out, ctx_out, sum_out):
     dim, seq = kT.shape
     c = (dim ** -0.5) * LOG2E
     here = pl.ds(pl.multiple_of(step * blk, blk), blk)
     q = qT[:, here]
     k_rows[here, :] = kT[:, here].T
 
-    def stats(i, carry, masked):
-        m, l = carry
+    def scores(i, masked):
         rows = pl.ds(pl.multiple_of(i * blk, blk), blk)
         s = dot(k_rows[rows, :], q) * c
         if masked:
             r = lax.broadcasted_iota(jnp.int32, (blk, blk), 0)
             col = lax.broadcasted_iota(jnp.int32, (blk, blk), 1)
             s = jnp.where(r <= col, s, -1e30)
-        s_buf[rows, :] = s
+        return s
+
+    def stats(i, carry, masked):
+        m, l = carry
+        s = scores(i, masked)
         new = jnp.maximum(m, jnp.max(s, axis=0, keepdims=True))
         l = l * jnp.exp2(m - new) + jnp.sum(jnp.exp2(s - new), axis=0, keepdims=True)
         return new, l
@@ -62,17 +65,17 @@
     m, l = stats(step, carry, True)
     lse = m + jnp.log2(l)
 
-    def apply(i, carry):
+    def apply(i, carry, masked):
         low_sum, res_sum = carry
-        rows = pl.ds(pl.multiple_of(i * blk, blk), blk)
-        p = jnp.exp2(s_buf[rows, :] - lse)
+        p = jnp.exp2(scores(i, masked) - lse)
         low = p.astype(BF16)
         res = (p - low.astype(F32)).astype(BF16)
-        v = vT[:, rows]
+        v = vT[:, pl.ds(pl.multiple_of(i * blk, blk), blk)]
         return low_sum + dot(v, low), res_sum + dot(v, res)
 
     zero = jnp.zeros((dim, blk), F32)
-    low_sum, res_sum = lax.fori_loop(0, step + 1, apply, (zero, zero))
+    carry = lax.fori_loop(0, step, functools.partial(apply, masked=False), (zero, zero))
+    low_sum, res_sum = apply(step, carry, True)
     ctx_out[:, here] = low_sum.astype(BF16)
     sum_out[:, here] = low_sum + res_sum
     lse_out[:, here] = jnp.broadcast_to(lse, (8, blk))
@@ -82,14 +85,6 @@
     dim, seq = kT.shape
     scale = dim ** -0.5
     c = scale * LOG2E
-
-    def turn(i, _):
-        cols = pl.ds(pl.multiple_of(i * blk, blk), blk)
-        k_rows[cols, :] = kT[:, cols].T
-        dk_acc[:, cols] = jnp.zeros((dim, blk), F32)
-        dv_acc[:, cols] = jnp.zeros((dim, blk), F32)
-        return 0
-    lax.fori_loop(0, seq // blk, turn, 0)
 
     def queries(step, _):
         here = pl.ds(pl.multiple_of(step * blk, blk), blk)
@@ -194,6 +189,11 @@
         at = self.buf.at[self.p.part(d, s, True, sub)]
         return remote(at, at, self.psend.at[d, s, sub], self.precv.at[d, s, sub], self.p.partner)
 
+    def first_way(self, d):
+        for sub in range(SUBS):
+            self.hop(d, 0, sub).start()
+            self.give(d, 0, sub).start()
+
     def first(self):
         for sub in range(SUBS):
             for d in (0, 1):
@@ -238,7 +238,7 @@
 
 
 class Scatter:
-    def __init__(self, place, own, keep, out, inc, send, recv, pout, pinc, psend, precv):
+    def __init__(self, place, own, keep, out, inc, pout, pinc, send, recv, psend, precv):
         self.p, self.own, self.keep, self.out, self.inc, self.send, self.recv = place, own, keep, out, inc, send, recv
         self.pout, self.pinc, self.psend, self.precv = pout, pinc, psend, precv
 
@@ -301,119 +301,22 @@
         lax.fori_loop(0, self.p.chips, one, 0)
 
 
-def gather_scratch(n, rows, width):
-    sems = [pltpu.SemaphoreType.DMA((2, n // 2, SUBS))] * 4
-    return [pltpu.VMEM((n * rows, width), BF16)] + sems
-
-
-def scatter_scratch(n, rows, width):
+def gather_sems(n):
+    return [pltpu.SemaphoreType.DMA((2, n // 2, SUBS))] * 4
+
+
+def scatter_sems(n):
+    sem = pltpu.SemaphoreType.DMA((2, n // 2))
+    fine = pltpu.SemaphoreType.DMA((2, n // 2, SUBS))
+    return [fine, fine, sem, sem]
+
+
+def scatter_bufs(n, rows, width):
     chips, half = n // 2, rows // 2
-    sem = pltpu.SemaphoreType.DMA((2, chips))
-    fine = pltpu.SemaphoreType.DMA((2, chips, SUBS))
     wide = pltpu.VMEM((2, half, width), F32)
     ring = pltpu.VMEM((2, chips - 1, half, width), BF16)
     pair = pltpu.VMEM((2, chips, half, width), BF16)
-    return [wide, wide, ring, ring, fine, fine, pair, pair, sem, sem]
-
-
-def mlp_kernel(n, dout_hbm, dout, x_mid, z, gain, bias, w1, w2, qT, kT, vT,
-               dw1_out, dw2_out, db1_out, dmid_out, vec_out, lse_out, ctx_out, sum_out, *scratch):
-    gy_s, gh_s, rs_s, (w1_t, w2_t, dw1_t, load_sem, k_rows, s_buf) = scratch[:5], scratch[5:10], scratch[10:20], scratch[20:]
-    place = Place(n, x_mid.shape[0])
-    half = place.half
-    blk = kT.shape[1] // place.chips
-    gy, gh, rs = Gather(place, *gy_s), Gather(place, *gh_s), Scatter(place, *rs_s)
-    mine = pl.ds(pl.multiple_of(place.me * place.rows, place.rows), place.rows)
-    load = pltpu.make_async_copy(dout_hbm, gy.buf.at[mine], load_sem)
-    load.start()
-    place.greet()
-    load.wait()
-    gy.first()
-    gh.buf[mine, :] = layer_norm_fwd(x_mid[...], gain[...], bias[...])[2]
-    w1_t[...] = w1[...].T
-    w2_t[...] = w2[...].T
-    dw1_t[...] = jnp.zeros_like(dw1_t)
-    dw2_out[...] = jnp.zeros_like(dw2_out)
-    db1_out[...] = jnp.zeros_like(db1_out)
-    gh.first()
-
-    def block(d, s, first):
-        gy.arrive(d, s)
-        dy = gy.load(d, s)
-        pre = jnp.concatenate([z[place.span(d, s, True), :], z[place.span(d, s, False), :]], axis=0).astype(F32)
-        act, slope = gelu_parts(pre)
-        dz = (dot(dy, w2_t[...]) * slope).astype(BF16)
-        rs.put(d, s, dot(dz, w1_t[...]), first)
-        if d == 1:
-            rs.give(0, s).start()
-        dw2_out[...] += dot(act.astype(BF16).T, dy)
-        db1_out[...] += jnp.sum(dz.astype(F32), axis=0, keepdims=True)
-        return dz
-
-    def late(d, s, dz):
-        gh.arrive(d, s)
-        dw1_t[...] += dot(dz.T, gh.load(d, s))
-
-    def attend(s):
-        attn_stats(s, blk, qT, kT, vT, k_rows, s_buf, lse_out, ctx_out, sum_out)
-
-    dz = [block(d, 0, True) for d in (0, 1)]
-    rs.give(1, 0).start()
-    for d in (0, 1):
-        late(d, 0, dz[d])
-    attend(0)
-
-    def step(s, _):
-        gy.pass_on(s)
-        dz = [block(d, s, False) for d in (0, 1)]
-        rs.give(1, s).start()
-        tail = rs.pass_on(s)
-        gh.pass_on(s)
-        tail.start()
-        for d in (0, 1):
-            late(d, s, dz[d])
-        attend(s)
-        return 0
-    lax.fori_loop(1, place.chips, step, 0)
-    dw1_out[...] = dw1_t[...].T
-
-    vec = jnp.zeros((4, x_mid.shape[1]), F32)
-    for d in (0, 1):
-        rows = slice(d * half, (d + 1) * half)
-        x_hat, inv_std, _ = layer_norm_fwd(x_mid[rows, :], gain[...], bias[...])
-        grad = rs.final(d, rs.keep)
-        dy = dout[rows, :].astype(F32)
-        dmid = (dy + layer_norm_bwd(grad, x_hat, inv_std, gain[...])).astype(BF16)
-        dmid_out[rows, :] = dmid
-        vec += jnp.concatenate([jnp.sum(a, axis=0, keepdims=True) for a in (grad * x_hat, grad, dmid.astype(F32), dy)], axis=0)
-    vec_out[...] = vec
-    for g in (gy, gh, rs):
-        g.drain()
-
-
-def comm_call(kernel, n, name, cid, args, out_shape, scratch, limit, hbm=()):
-    vm = pl.BlockSpec(memory_space=pltpu.VMEM)
-    return pl.pallas_call(
-        functools.partial(kernel, n),
-        in_specs=[pl.BlockSpec(memory_space=pl.ANY) if i in hbm else vm for i in range(len(args))],
-        out_specs=[vm] * len(out_shape),
-        out_shape=[jax.ShapeDtypeStruct(*o) for o in out_shape],
-        scratch_shapes=scratch,
-        compiler_params=pltpu.CompilerParams(collective_id=cid, has_side_effects=True, vmem_limit_bytes=limit << 20),
-        name=name,
-    )(*args)
-
-
-def mlp_stage(n, dout, x_mid, z, gain, bias, w1, w2, q_t, k_t, v_t):
-    rows, width = dout.shape
-    units = z.shape[1]
-    dim, seq = q_t.shape
-    scratch = gather_scratch(n, rows, width) * 2 + scatter_scratch(n, rows, width) + [
-        pltpu.VMEM((units, width), BF16), pltpu.VMEM((width, units), BF16), pltpu.VMEM((units, width), F32), pltpu.SemaphoreType.DMA,
-        pltpu.VMEM((seq, dim), BF16), pltpu.VMEM((seq, 2 * seq // n), F32)]
-    return comm_call(mlp_kernel, n, "mlp_stage", 1, (dout, dout, x_mid, z, gain, bias, w1, w2, q_t, k_t, v_t),
-                     [((width, units), F32), ((units, width), F32), ((1, units), F32), ((rows, width), BF16), ((4, width), F32),
-                      ((8, seq), F32), ((dim, seq), BF16), ((dim, seq), F32)], scratch, 63, hbm=(0,))
+    return [wide, wide, ring, ring, pair, pair]
 
 
 class Spread:
@@ -446,30 +349,104 @@
         lax.fori_loop(1, self.p.n, one, 0)
 
 
-def attn_kernel(n, dmid_hbm, dmid, ctx_t, ctx_sum, lse, qT, kT, vT, wo, x_in, early, gain, bias, w_t,
-                dwo_out, dx_out, dw_out, db_out, vec_out, *scratch):
-    g_s, gh_s, rs_s = scratch[:5], scratch[5:10], scratch[10:20]
-    load_sem, dctx, dqkv_t, k_rows, dk_acc, dv_acc, late_part, e_buf, e_send, e_recv, l_buf, l_send, l_recv = scratch[20:]
-    place = Place(n, x_in.shape[0])
+def layer_kernel(n, loads, *refs):
+    hbm, refs = refs[:loads], refs[loads:]
+    gain2, bias2, gain1, bias1, dw1_out, dw2_out, db1_out, dwo_out, dx_out, dw_out, db_out, vec_out = refs[:12]
+    x_mid, z, w1, w2, qT, kT, vT, wo, x_in, w_t = refs[12:12 + loads - 1]
+    scratch = refs[12 + loads - 1:]
+    load_sems, gy_buf, gh_buf = scratch[:3]
+    rs_bufs, gathers, scatters, rest = scratch[3:9], scratch[9:25], scratch[25:33], scratch[33:]
+    w1_t, w2_t, dw1_t, k_rows, lse, ctx_t, ctx_sum, dctx, dqkv_t, dk_acc, dv_acc, early, late_part, e_buf, e_send, e_recv, l_buf, l_send, l_recv = rest
+    rows_here, width = x_mid.shape
+    place = Place(n, rows_here)
     half, chips = place.half, place.chips
     seq = kT.shape[1]
     blk = seq // chips
-    g, gh, rs = Gather(place, *g_s), Gather(place, *gh_s), Scatter(place, *rs_s)
+    gy, gh, gm, g1 = (Gather(place, buf, *gathers[4 * i:4 * i + 4]) for i, buf in enumerate((gy_buf, gh_buf, gy_buf, gh_buf)))
+    rs2, rs1 = (Scatter(place, *rs_bufs, *scatters[4 * i:4 * i + 4]) for i in range(2))
     first_rows, last_rows = Spread(place, early, e_buf, e_send, e_recv), Spread(place, late_part, l_buf, l_send, l_recv)
-    mine = pl.ds(pl.multiple_of(place.me * place.rows, place.rows), place.rows)
-    load = pltpu.make_async_copy(dmid_hbm, g.buf.at[mine], load_sem)
-    load.start()
+    mine = pl.ds(pl.multiple_of(place.me * rows_here, rows_here), rows_here)
+    way = [pl.ds(pl.multiple_of(place.me * rows_here + d * half, half), half) for d in (0, 1)]
+
+    copies = [pltpu.make_async_copy(hbm[0], gy_buf.at[mine], load_sems.at[0])]
+    copies += [pltpu.make_async_copy(hbm[i], refs[11 + i], load_sems.at[i]) for i in range(1, loads)]
+    for c in copies:
+        c.start()
     place.greet_all()
-    load.wait()
-    g.first()
-    gh.buf[mine, :] = layer_norm_fwd(x_in[...], gain[...], bias[...])[2]
-    dwo_out[...] = jnp.zeros_like(dwo_out)
-    dw_out[...] = jnp.zeros_like(dw_out)
-    db_out[...] = jnp.zeros_like(db_out)
+    copies[0].wait()
+    gy.first()
+    for c in copies[1:]:
+        c.wait()
+    gh_buf[mine, :] = layer_norm_fwd(x_mid[...], gain2[...], bias2[...])[2]
+    w1_t[...] = w1[...].T
+    w2_t[...] = w2[...].T
+    for acc in (dw1_t, dw2_out, db1_out, dwo_out, dw_out, db_out, dk_acc, dv_acc):
+        acc[...] = jnp.zeros_like(acc)
+    gh.first()
+
+    def block(d, s, first):
+        gy.arrive(d, s)
+        dy = gy.load(d, s)
+        pre = jnp.concatenate([z[place.span(d, s, True), :], z[place.span(d, s, False), :]], axis=0).astype(F32)
+        act, slope = gelu_parts(pre)
+        dz = (dot(dy, w2_t[...]) * slope).astype(BF16)
+        rs2.put(d, s, dot(dz, w1_t[...]), first)
+        if d == 1:
+            rs2.give(0, s).start()
+        dw2_out[...] += dot(act.astype(BF16).T, dy)
+        db1_out[...] += jnp.sum(dz.astype(F32), axis=0, keepdims=True)
+        return dz
+
+    def late(d, s, dz):
+        gh.arrive(d, s)
+        dw1_t[...] += dot(dz.T, gh.load(d, s))
+
+    def attend(s):
+        attn_stats(s, blk, qT, kT, vT, k_rows, lse, ctx_t, ctx_sum)
+
+    dz = [block(d, 0, True) for d in (0, 1)]
+    rs2.give(1, 0).start()
+    for d in (0, 1):
+        late(d, 0, dz[d])
+    attend(0)
+
+    def mlp_step(s, _):
+        gy.pass_on(s)
+        dz = [block(d, s, False) for d in (0, 1)]
+
+        @pl.when(s == chips - 1)
+        def _():
+            gy.drain()
+        rs2.give(1, s).start()
+        tail = rs2.pass_on(s)
+        gh.pass_on(s)
+        tail.start()
+        for d in (0, 1):
+            late(d, s, dz[d])
+        attend(s)
+        return 0
+    lax.fori_loop(1, chips, mlp_step, 0)
+    gh.drain()
+
+    for d in (0, 1):
+        rs2.own[d] = rs2.final(d, rs2.keep)
+    vec = jnp.zeros((4, width), F32)
+    for d in (0, 1):
+        rows = slice(d * half, (d + 1) * half)
+        x_hat, inv_std, _ = layer_norm_fwd(x_mid[rows, :], gain2[...], bias2[...])
+        grad = rs2.own[d]
+        dy = gy_buf[way[d], :].astype(F32)
+        dmid = (dy + layer_norm_bwd(grad, x_hat, inv_std, gain2[...])).astype(BF16)
+        gy_buf[way[d], :] = dmid
+        vec += jnp.concatenate([jnp.sum(a, axis=0, keepdims=True) for a in (grad * x_hat, grad, dmid.astype(F32), dy)], axis=0)
+        gm.first_way(d)
+    early[...] = vec
+    rs2.drain()
+    gh_buf[mine, :] = layer_norm_fwd(x_in[...], gain1[...], bias1[...])[2]
 
     def project(d, s):
-        g.arrive(d, s)
-        rows = g.load(d, s)
+        gm.arrive(d, s)
+        rows = gm.load(d, s)
         both = dot_nt(wo[...], rows).astype(BF16)
         cols = [place.span(d, s, own) for own in (True, False)]
         dctx[:, cols[0]] = both[:, :half]
@@ -478,95 +455,134 @@
 
     for d in (0, 1):
         project(d, 0)
+    dw1_out[...] = dw1_t[...].T
 
     def mid_step(s, _):
-        g.pass_on(s)
+        gm.pass_on(s)
         for d in (0, 1):
             project(d, s)
         return 0
     lax.fori_loop(1, chips - 1, mid_step, 0)
-    g.pass_on(chips - 1)
-    gh.first()
+    gm.pass_on(chips - 1)
+    g1.first()
     first_rows.start()
     for d in (0, 1):
         project(d, chips - 1)
 
     stride = 3
     blocks = chips * (chips + 1) // 2
-    done = (blocks + stride - 1) // stride
     events = SUBS * (chips - 1)
+    left = list(range((blocks + stride - 1) // stride, events))
+
+    def event(ev):
+        g1.pass_one(1 + ev // SUBS, ev % SUBS if isinstance(ev, int) else lax.rem(ev, SUBS))
 
     def service(e):
         ev = e // stride
 
         @pl.when((lax.rem(e, stride) == 0) & (ev < events))
         def _():
-            gh.pass_one(1 + ev // SUBS, lax.rem(ev, SUBS))
+            event(ev)
 
     attn_grads(blk, qT, kT, vT, dctx, lse, ctx_sum, dqkv_t, k_rows, dk_acc, dv_acc, service)
 
     def cols_of(d, s):
         return jnp.concatenate([dqkv_t[:, place.span(d, s, own)] for own in (True, False)], axis=1)
 
-    def block(s):
+    def back(s):
         for d in (0, 1):
-            rs.put(d, s, dot(cols_of(d, s).T, w_t[...]))
+            rows = cols_of(d, s).T
+            rs1.put(d, s, dot(rows, w_t[...]))
             if d == 1:
-                rs.give(0, s).start()
-
-    def late(d, s):
-        gh.arrive(d, s)
-        cols = cols_of(d, s)
-        dw_out[...] += dot(cols, gh.load(d, s))
-        db_out[...] += jnp.sum(cols.astype(F32), axis=1, keepdims=True)
-
-    block(1)
-    rs.give(1, 1).start()
-
-    def step(s, _):
-        tail = rs.pass_on(s)
+                rs1.give(0, s).start()
+            db_out[...] += jnp.sum(rows.astype(F32), axis=0, keepdims=True)
+
+    def weigh(d, s):
+        g1.arrive(d, s)
+        dw_out[...] += dot(cols_of(d, s), g1.load(d, s))
+
+    for ev in left[:1]:
+        event(ev)
+    back(1)
+    rs1.give(1, 1).start()
+    for ev in left[1:]:
+        event(ev)
+
+    def qkv_step(s, _):
+        tail = rs1.pass_on(s)
         following = lax.rem(s + 1, chips)
-        block(following)
+        back(following)
         tail.start()
-        rs.give(1, following).start()
-        ev = done + s - 2
-
-        @pl.when((s >= 2) & (ev < events))
-        def _():
-            gh.pass_one(1 + ev // SUBS, lax.rem(ev, SUBS))
+        rs1.give(1, following).start()
         for d in (0, 1):
-            late(d, s - 1)
+            weigh(d, s - 1)
         return 0
-    lax.fori_loop(1, chips, step, 0)
-
-    vec = jnp.zeros((2, x_in.shape[1]), F32)
+    lax.fori_loop(1, chips, qkv_step, 0)
+
+    vec = jnp.zeros((2, width), F32)
     for d in (0, 1):
         rows = slice(d * half, (d + 1) * half)
-        x_hat, inv_std, _ = layer_norm_fwd(x_in[rows, :], gain[...], bias[...])
-        grad = rs.final(d, rs.own)
-        dx_out[rows, :] = (dmid[rows, :].astype(F32) + layer_norm_bwd(grad, x_hat, inv_std, gain[...])).astype(BF16)
+        x_hat, inv_std, _ = layer_norm_fwd(x_in[rows, :], gain1[...], bias1[...])
+        grad = rs1.final(d, rs1.own)
+        dx_out[rows, :] = (gy_buf[way[d], :].astype(F32) + layer_norm_bwd(grad, x_hat, inv_std, gain1[...])).astype(BF16)
         vec += jnp.concatenate([jnp.sum(grad * x_hat, axis=0, keepdims=True), jnp.sum(grad, axis=0, keepdims=True)], axis=0)
     late_part[...] = vec
     vec_out[2:6, :] = first_rows.total()
     last_rows.start()
     for d in (0, 1):
-        late(d, chips - 1)
+        weigh(d, chips - 1)
     vec_out[0:2, :] = last_rows.total()
-    for one in (g, gh, rs, first_rows, last_rows):
+    for one in (gm, g1, rs1, first_rows, last_rows):
         one.drain()
 
 
-def attn_stage(n, dmid, ctx_t, ctx_sum, lse, q_t, k_t, v_t, wo, x_in, early, gain, bias, w_t):
-    rows, width = x_in.shape
+def layer_stage(n, dout, x_mid, z, w1, w2, q_t, k_t, v_t, wo, x_in, w_t, gain2, bias2, gain1, bias1):
+    rows, width = dout.shape
+    units = z.shape[1]
     dim, seq = q_t.shape
+    hbm = (dout, x_mid, z, w1, w2, q_t, k_t, v_t, wo, x_in, w_t)
+    vm = pl.BlockSpec(memory_space=pltpu.VMEM)
+    full = pltpu.VMEM((n * rows, width), BF16)
     sem = pltpu.SemaphoreType.DMA((n,))
     acc = pltpu.VMEM((dim, seq), F32)
-    scratch = gather_scratch(n, rows, width) * 2 + scatter_scratch(n, rows, width) + [
-        pltpu.SemaphoreType.DMA, pltpu.VMEM((dim, seq), BF16), pltpu.VMEM((3 * dim, seq), BF16), pltpu.VMEM((seq, dim), BF16), acc, acc,
-        pltpu.VMEM((2, width), F32), pltpu.VMEM((n, 4, width), F32), sem, sem, pltpu.VMEM((n, 2, width), F32), sem, sem]
-    return comm_call(attn_kernel, n, "attn_stage", 2,
-                     (dmid, dmid, ctx_t, ctx_sum, lse, q_t, k_t, v_t, wo, x_in, early, gain, bias, w_t),
-                     [((dim, width), F32), ((rows, width), BF16), (w_t.shape, F32), ((3 * dim, 1), F32), ((6, width), F32)], scratch, 63, hbm=(0,))
+    scratch = [pltpu.VMEM(a.shape, a.dtype) for a in hbm[1:]] + [pltpu.SemaphoreType.DMA((len(hbm),)), full, full]
+    scratch += scatter_bufs(n, rows, width) + gather_sems(n) * 4 + scatter_sems(n) * 2
+    scratch += [pltpu.VMEM((units, width), BF16), pltpu.VMEM((width, units), BF16), pltpu.VMEM((units, width), F32),
+                pltpu.VMEM((seq, dim), BF16), pltpu.VMEM((8, seq), F32), pltpu.VMEM((dim, seq), BF16), acc,
+                pltpu.VMEM((dim, seq), BF16), pltpu.VMEM((3 * dim, seq), BF16), acc, acc,
+                pltpu.VMEM((4, width), F32), pltpu.VMEM((2, width), F32),
+                pltpu.VMEM((n, 4, width), F32), sem, sem, pltpu.VMEM((n, 2, width), F32), sem, sem]
+    outs = [((width, units), F32), ((units, width), F32), ((1, units), F32), ((dim, width), F32), ((rows, width), BF16),
+            (w_t.shape, F32), ((1, 3 * dim), F32), ((6, width), F32)]
+    return pl.pallas_call(
+        functools.partial(layer_kernel, n, len(hbm)),
+        in_specs=[pl.BlockSpec(memory_space=pl.ANY)] * len(hbm) + [vm] * 4,
+        out_specs=[vm] * len(outs),
+        out_shape=[jax.ShapeDtypeStruct(*o) for o in outs],
+        scratch_shapes=scratch,
+        compiler_params=pltpu.CompilerParams(collective_id=1, has_side_effects=True, vmem_limit_bytes=67043328),
+        name="layer_stage",
+    )(*hbm, gain2, bias2, gain1, bias1)
+
+
+def deliver_kernel(count, *refs):
+    for i in range(count):
+        refs[count + i][...] = refs[i][...]
+
+
+def deliver(big, small, steps=4):
+    cut = [pl.BlockSpec((a.shape[0] // steps, a.shape[1]), lambda i: (i, 0)) for a in big]
+    whole = [pl.BlockSpec(a.shape, lambda i: (0, 0)) for a in small]
+    args = list(big) + list(small)
+    return pl.pallas_call(
+        functools.partial(deliver_kernel, len(args)),
+        grid=(steps,),
+        in_specs=cut + whole,
+        out_specs=cut + whole,
+        out_shape=[jax.ShapeDtypeStruct(a.shape, a.dtype) for a in args],
+        compiler_params=pltpu.CompilerParams(dimension_semantics=("arbitrary",), vmem_limit_bytes=67043328),
+        name="deliver",
+    )(*args)
 
 
 def solution(mesh):
@@ -575,13 +591,13 @@
         dim = q_saved.shape[-1]
         row = lambda a: a[None, :]
         q_t, k_t, v_t = (jnp.transpose(a[0, :, 0, :]) for a in (q_saved, k_saved, v_saved))
-        grad_wfc1, grad_wfc2, grad_bfc1, grad_mid, early, lse, ctx_t, ctx_sum = mlp_stage(
-            n, d_out[0], x_mid[0], z_saved[0], row(ln2_gain), row(ln2_bias), w_fc1, w_fc2, q_t, k_t, v_t)
         w_qkv_t = jnp.transpose(w_qkv[:, :, 0, :], (0, 2, 1)).reshape(3 * dim, -1)
-        grad_wproj, grad_x, grad_w_t, grad_b, grad_vecs = attn_stage(
-            n, grad_mid, ctx_t, ctx_sum, lse, q_t, k_t, v_t, w_proj[0], x_in[0], early, row(ln1_gain), row(ln1_bias), w_qkv_t)
-        grad_wqkv = jnp.transpose(grad_w_t.reshape(3, dim, -1), (0, 2, 1))[:, :, None, :]
-        return grad_x[None], grad_wqkv, grad_b.reshape(3, 1, dim), grad_wproj[None], grad_wfc1, grad_bfc1[0], grad_wfc2, grad_vecs
+        dw1, dw2, db1, dwo, dx, dw_t, db, vecs = layer_stage(
+            n, d_out[0], x_mid[0], z_saved[0], w_fc1, w_fc2, q_t, k_t, v_t, w_proj[0], x_in[0], w_qkv_t,
+            row(ln2_gain), row(ln2_bias), row(ln1_gain), row(ln1_bias))
+        dx, dw_t, dwo, dw1, dw2, db1, db, vecs = deliver((dx, dw_t, dwo, dw1, dw2), (db1, db, vecs))
+        grad_wqkv = jnp.transpose(dw_t.reshape(3, dim, -1), (0, 2, 1))[:, :, None, :]
+        return dx[None], grad_wqkv, db.reshape(3, 1, dim), dwo[None], dw1, db1[0], dw2, vecs
 
     tok_spec = P('dp', 'tp', None)
     head_spec = P('dp', None, 'tp', None)

time: 305 us -> 294 us (0.964)
  local copies, waits for them, and re-layouts: 8.54 us -> 1.24 us
  Pallas kernels: 295 us -> 290 us
    unnamed x17 -> x0, local copies, waits for them, and re-layouts: 7.88 us -> none
    pallas_call x2, Pallas kernels: 295 us -> 290 us  [the longest x1 286 us: layer_stage(): pl.pallas_call(functools.partial(layer_kernel, n, len(hbm)), in_specs=[pl...]
where the time goes in v4:
time: 294 us; the launch traced here: 293 us
  Pallas kernels  290 us (99%)
    pallas_call x1, Pallas kernels, layer_stage(): pl.pallas_call(functools.partial(layer_kernel, n, len(hbm)), in_specs=[pl...  286 us

profile of v4, /device:TPU:21, one launch (start us, length us, event | category | flops | bytes accessed | tf_op | source)
XLA Modules:
  0.0 293.4 jit_solution(16750513368066948204)
XLA Ops:
  0.6 285.7 %layer_stage.1 = (f32[1024,256]{1,0:T(8,128)}, f32[256,1024]{1,0:T(8,128)}, f32[1,256]{1,0:T(1,128)}, f32[64,1024]{1,0:T(8,128)}, bf16[256,1024]{1,0:T(8,128)(2,...) custom-call(bf16[256,1024]{1,0:T(8,128)(2,1)} %bitcast.32, bf16[256,1024]{1,0:T(8,128)(2,1)} %bitcast.33, ...), custom_call_target="tpu_custom_call" | custom-call | tf_op jit(solution)/shard_map/layer_stage/pallas_call | solution.py:557
  286.3 4.5 %deliver.1 = (bf16[256,1024]{1,0:T(8,128)(2,1)}, f32[192,1024]{1,0:T(8,128)}, f32[64,1024]{1,0:T(8,128)}, f32[1024,256]{1,0:T(8,128)}, f32[256,1024]{1,0:T(8,128...) custom-call(bf16[256,1024]{1,0:T(8,128)(2,1)} %get-tuple-element.24.refs_0_, ...), custom_call_target="tpu_custom_call" | custom-call | tf_op jit(solution)/shard_map/deliver/pallas_call | solution.py:577
  290.8 0.6 broadcast.3
  291.4 1.4 reduce.3
  292.8 0.6 reshape.28

commit v5 on v4

--- a/solution.py
+++ b/solution.py
@@ -146,7 +146,6 @@
         self.core, self.chip = lax.rem(me, 2), me // 2
         self.partner = me + 1 - 2 * self.core
         self.next = (lax.rem(me + 2, n), lax.rem(me + n - 2, n))
-        self.sub = self.half // SUBS
 
     def origin(self, d, s):
         return lax.rem(self.chip + (self.chips - s if d == 0 else s), self.chips)
@@ -156,10 +155,10 @@
         start = (2 * self.origin(d, s) + core) * self.rows + d * self.half
         return pl.ds(pl.multiple_of(start, self.half), self.half)
 
-    def part(self, d, s, own, sub):
-        core = self.core if own else 1 - self.core
-        start = (2 * self.origin(d, s) + core) * self.rows + d * self.half + sub * self.sub
-        return pl.ds(pl.multiple_of(start, self.sub), self.sub)
+    def part(self, d, s, own, sub, subs):
+        core, size = self.core if own else 1 - self.core, self.half // subs
+        start = (2 * self.origin(d, s) + core) * self.rows + d * self.half + sub * size
+        return pl.ds(pl.multiple_of(start, size), size)
 
     def greet(self):
         barrier = pltpu.get_barrier_semaphore()
@@ -178,33 +177,33 @@
 
 
 class Gather:
-    def __init__(self, place, buf, send, recv, psend, precv):
-        self.p, self.buf, self.send, self.recv, self.psend, self.precv = place, buf, send, recv, psend, precv
+    def __init__(self, subs, place, buf, send, recv, psend, precv):
+        self.subs, self.p, self.buf, self.send, self.recv, self.psend, self.precv = subs, place, buf, send, recv, psend, precv
 
     def hop(self, d, s, sub):
-        at = self.buf.at[self.p.part(d, s, True, sub)]
+        at = self.buf.at[self.p.part(d, s, True, sub, self.subs)]
         return remote(at, at, self.send.at[d, s, sub], self.recv.at[d, s, sub], self.p.next[d])
 
     def give(self, d, s, sub):
-        at = self.buf.at[self.p.part(d, s, True, sub)]
+        at = self.buf.at[self.p.part(d, s, True, sub, self.subs)]
         return remote(at, at, self.psend.at[d, s, sub], self.precv.at[d, s, sub], self.p.partner)
 
     def first_way(self, d):
-        for sub in range(SUBS):
+        for sub in range(self.subs):
             self.hop(d, 0, sub).start()
             self.give(d, 0, sub).start()
 
     def first(self):
-        for sub in range(SUBS):
+        for sub in range(self.subs):
             for d in (0, 1):
                 self.hop(d, 0, sub).start()
-        for sub in range(SUBS):
+        for sub in range(self.subs):
             for d in (0, 1):
                 self.give(d, 0, sub).start()
 
     def pass_one(self, s, sub):
         for d in (0, 1):
-            at = self.buf.at[self.p.part(d, s, True, sub)]
+            at = self.buf.at[self.p.part(d, s, True, sub, self.subs)]
             remote(at, at, self.send.at[d, s - 1, sub], self.recv.at[d, s - 1, sub], self.p.next[d]).wait_recv()
 
             @pl.when(s < self.p.chips - 1)
@@ -213,12 +212,12 @@
             self.give(d, s, sub).start()
 
     def pass_on(self, s):
-        for sub in range(SUBS):
+        for sub in range(self.subs):
             self.pass_one(s, sub)
 
     def arrive(self, d, s):
-        for sub in range(SUBS):
-            at = self.buf.at[self.p.part(d, s, False, sub)]
+        for sub in range(self.subs):
+            at = self.buf.at[self.p.part(d, s, False, sub, self.subs)]
             remote(at, at, self.psend.at[d, s, sub], self.precv.at[d, s, sub], self.p.partner).wait_recv()
 
     def load(self, d, s):
@@ -227,7 +226,7 @@
     def drain(self):
         def one(s, _):
             for d in (0, 1):
-                for sub in range(SUBS):
+                for sub in range(self.subs):
                     self.give(d, s, sub).wait_send()
 
                     @pl.when(s < self.p.chips - 1)
@@ -238,7 +237,8 @@
 
 
 class Scatter:
-    def __init__(self, place, own, keep, out, inc, pout, pinc, send, recv, psend, precv):
+    def __init__(self, subs, place, own, keep, out, inc, pout, pinc, send, recv, psend, precv):
+        self.subs, self.size = subs, place.half // subs
         self.p, self.own, self.keep, self.out, self.inc, self.send, self.recv = place, own, keep, out, inc, send, recv
         self.pout, self.pinc, self.psend, self.precv = pout, pinc, psend, precv
 
@@ -246,7 +246,7 @@
         return remote(self.pout.at[d, s], self.pinc.at[d, s], self.psend.at[d, s], self.precv.at[d, s], self.p.partner)
 
     def hop(self, d, r, sub):
-        rows = slice(sub * self.p.sub, (sub + 1) * self.p.sub)
+        rows = slice(sub * self.size, (sub + 1) * self.size)
         return remote(self.out.at[d, r, rows], self.inc.at[d, r, rows], self.send.at[d, r, sub], self.recv.at[d, r, sub], self.p.next[d])
 
     def put(self, d, s, part, first=False):
@@ -259,7 +259,7 @@
         self.own[d] += self.pinc[d, s].astype(F32)
 
     def forward(self, d, s, sub):
-        rows = slice(sub * self.p.sub, (sub + 1) * self.p.sub)
+        rows = slice(sub * self.size, (sub + 1) * self.size)
 
         @pl.when(s >= 2)
         def _():
@@ -274,7 +274,7 @@
         for d in (0, 1):
             self.join(d, s)
         before = None
-        for sub in range(SUBS):
+        for sub in range(self.subs):
             for d in (0, 1):
                 self.forward(d, s, sub)
                 if before is not None:
@@ -285,7 +285,7 @@
     def final(self, d, store):
         last = self.p.chips - 2
         self.give(d, 0).wait_recv()
-        for sub in range(SUBS):
+        for sub in range(self.subs):
             self.hop(d, last, sub).wait_recv()
         return store[d] + self.pinc[d, 0].astype(F32) + self.inc[d, last].astype(F32)
 
@@ -293,7 +293,7 @@
         def one(s, _):
             for d in (0, 1):
                 self.give(d, s).wait_send()
-                for sub in range(SUBS):
+                for sub in range(self.subs):
                     @pl.when(s < self.p.chips - 1)
                     def _():
                         self.hop(d, s, sub).wait_send()
@@ -349,22 +349,78 @@
         lax.fori_loop(1, self.p.n, one, 0)
 
 
+class PairSpread:
+    def __init__(self, place, part, other, half, buf, total, swap, pair_sems, send, recv):
+        self.p, self.part, self.other, self.half, self.buf, self.sum, self.swap = place, part, other, half, buf, total, swap
+        self.pair_sems, self.send, self.recv = pair_sems, send, recv
+        self.rows = part.shape[0] // 2
+
+    def pair(self, src, dst, i):
+        return remote(src, dst, self.pair_sems.at[0, i], self.pair_sems.at[1, i], self.p.partner)
+
+    def to(self, r):
+        p = self.p
+        return remote(self.half, self.buf.at[p.chip], self.send.at[r], self.recv.at[p.chip], lax.rem(p.me + 2 * r, p.n))
+
+    def start(self):
+        self.pair(self.part, self.other, 0).start()
+
+    def across(self):
+        self.pair(self.part, self.other, 0).wait_recv()
+        both = self.part[...] + self.other[...]
+        half = jnp.where(self.p.core == 0, both[:self.rows], both[self.rows:])
+        self.half[...] = half
+        self.buf[pl.ds(self.p.chip, 1)] = half[None]
+
+        def one(r, _):
+            self.to(r).start()
+            return 0
+        lax.fori_loop(1, self.p.chips, one, 0)
+
+    def back(self):
+        p = self.p
+
+        def one(r, _):
+            src = lax.rem(p.chip + p.chips - r, p.chips)
+            remote(self.half, self.buf.at[src], self.send.at[r], self.recv.at[src], lax.rem(p.me + p.n - 2 * r, p.n)).wait_recv()
+            return 0
+        lax.fori_loop(1, p.chips, one, 0)
+        self.sum[...] = lax.fori_loop(1, p.chips, lambda j, acc: acc + self.buf[j], self.buf[0])
+        self.pair(self.sum, self.swap, 1).start()
+
+    def total(self):
+        self.pair(self.sum, self.swap, 1).wait_recv()
+        mine, its = self.sum[...], self.swap[...]
+        low = self.p.core == 0
+        return jnp.concatenate([jnp.where(low, mine, its), jnp.where(low, its, mine)], axis=0)
+
+    def drain(self):
+        self.pair(self.part, self.other, 0).wait_send()
+        self.pair(self.sum, self.swap, 1).wait_send()
+
+        def one(r, _):
+            self.to(r).wait_send()
+            return 0
+        lax.fori_loop(1, self.p.chips, one, 0)
+
+
 def layer_kernel(n, loads, *refs):
     hbm, refs = refs[:loads], refs[loads:]
-    gain2, bias2, gain1, bias1, dw1_out, dw2_out, db1_out, dwo_out, dx_out, dw_out, db_out, vec_out = refs[:12]
+    gain2, bias2, gain1, bias1, dw1_hbm, dw2_hbm, db1_out, dwo_hbm, dx_out, dw_out, db_out, vec_out = refs[:12]
     x_mid, z, w1, w2, qT, kT, vT, wo, x_in, w_t = refs[12:12 + loads - 1]
     scratch = refs[12 + loads - 1:]
     load_sems, gy_buf, gh_buf = scratch[:3]
     rs_bufs, gathers, scatters, rest = scratch[3:9], scratch[9:25], scratch[25:33], scratch[33:]
-    w1_t, w2_t, dw1_t, k_rows, lse, ctx_t, ctx_sum, dctx, dqkv_t, dk_acc, dv_acc, early, late_part, e_buf, e_send, e_recv, l_buf, l_send, l_recv = rest
+    w1_t, w2_t, dw1_t, k_rows, lse, ctx_t, ctx_sum, dctx, dqkv_t, dk_acc, dv_acc, early, late_part = rest[:13]
+    e_refs, (l_buf, l_send, l_recv), (dw1_out, dw2_out, dwo_out, db_acc, out_sems) = rest[13:21], rest[21:24], rest[24:]
     rows_here, width = x_mid.shape
     place = Place(n, rows_here)
     half, chips = place.half, place.chips
     seq = kT.shape[1]
     blk = seq // chips
-    gy, gh, gm, g1 = (Gather(place, buf, *gathers[4 * i:4 * i + 4]) for i, buf in enumerate((gy_buf, gh_buf, gy_buf, gh_buf)))
-    rs2, rs1 = (Scatter(place, *rs_bufs, *scatters[4 * i:4 * i + 4]) for i in range(2))
-    first_rows, last_rows = Spread(place, early, e_buf, e_send, e_recv), Spread(place, late_part, l_buf, l_send, l_recv)
+    gy, gh, gm, g1 = (Gather(subs, place, buf, *gathers[4 * i:4 * i + 4]) for i, (subs, buf) in enumerate(((1, gy_buf), (1, gh_buf), (SUBS, gy_buf), (SUBS, gh_buf))))
+    rs2, rs1 = (Scatter(subs, place, *rs_bufs, *scatters[4 * i:4 * i + 4]) for i, subs in enumerate((1, SUBS)))
+    first_rows, last_rows = PairSpread(place, early, *e_refs), Spread(place, late_part, l_buf, l_send, l_recv)
     mine = pl.ds(pl.multiple_of(place.me * rows_here, rows_here), rows_here)
     way = [pl.ds(pl.multiple_of(place.me * rows_here + d * half, half), half) for d in (0, 1)]
 
@@ -380,7 +436,7 @@
     gh_buf[mine, :] = layer_norm_fwd(x_mid[...], gain2[...], bias2[...])[2]
     w1_t[...] = w1[...].T
     w2_t[...] = w2[...].T
-    for acc in (dw1_t, dw2_out, db1_out, dwo_out, dw_out, db_out, dk_acc, dv_acc):
+    for acc in (dw1_t, dw2_out, db1_out, dwo_out, dw_out, db_acc, dk_acc, dv_acc):
         acc[...] = jnp.zeros_like(acc)
     gh.first()
 
@@ -442,6 +498,7 @@
         gm.first_way(d)
     early[...] = vec
     rs2.drain()
+    first_rows.start()
     gh_buf[mine, :] = layer_norm_fwd(x_in[...], gain1[...], bias1[...])[2]
 
     def project(d, s):
@@ -456,6 +513,8 @@
     for d in (0, 1):
         project(d, 0)
     dw1_out[...] = dw1_t[...].T
+    leave = [pltpu.make_async_copy(a, b, out_sems.at[i]) for i, (a, b) in enumerate(((dw2_out, dw2_hbm), (dw1_out, dw1_hbm), (dwo_out, dwo_hbm)))]
+    leave[0].start()
 
     def mid_step(s, _):
         gm.pass_on(s)
@@ -465,17 +524,19 @@
     lax.fori_loop(1, chips - 1, mid_step, 0)
     gm.pass_on(chips - 1)
     g1.first()
-    first_rows.start()
+    first_rows.across()
+    leave[1].start()
     for d in (0, 1):
         project(d, chips - 1)
 
     stride = 3
     blocks = chips * (chips + 1) // 2
-    events = SUBS * (chips - 1)
+    events = g1.subs * (chips - 1)
+    leave[2].start()
     left = list(range((blocks + stride - 1) // stride, events))
 
     def event(ev):
-        g1.pass_one(1 + ev // SUBS, ev % SUBS if isinstance(ev, int) else lax.rem(ev, SUBS))
+        g1.pass_one(1 + ev // g1.subs, ev % g1.subs if isinstance(ev, int) else lax.rem(ev, g1.subs))
 
     def service(e):
         ev = e // stride
@@ -495,7 +556,7 @@
             rs1.put(d, s, dot(rows, w_t[...]))
             if d == 1:
                 rs1.give(0, s).start()
-            db_out[...] += jnp.sum(rows.astype(F32), axis=0, keepdims=True)
+            db_acc[...] += jnp.sum(rows.astype(F32), axis=0, keepdims=True)
 
     def weigh(d, s):
         g1.arrive(d, s)
@@ -507,6 +568,7 @@
     rs1.give(1, 1).start()
     for ev in left[1:]:
         event(ev)
+    first_rows.back()
 
     def qkv_step(s, _):
         tail = rs1.pass_on(s)
@@ -532,8 +594,13 @@
     for d in (0, 1):
         weigh(d, chips - 1)
     vec_out[0:2, :] = last_rows.total()
+    dim = qT.shape[0]
+    for i in range(3):
+        db_out[i] = db_acc[:, i * dim:(i + 1) * dim]
     for one in (gm, g1, rs1, first_rows, last_rows):
         one.drain()
+    for c in leave:
+        c.wait()
 
 
 def layer_stage(n, dout, x_mid, z, w1, w2, q_t, k_t, v_t, wo, x_in, w_t, gain2, bias2, gain1, bias1):
@@ -551,13 +618,17 @@
                 pltpu.VMEM((seq, dim), BF16), pltpu.VMEM((8, seq), F32), pltpu.VMEM((dim, seq), BF16), acc,
                 pltpu.VMEM((dim, seq), BF16), pltpu.VMEM((3 * dim, seq), BF16), acc, acc,
                 pltpu.VMEM((4, width), F32), pltpu.VMEM((2, width), F32),
-                pltpu.VMEM((n, 4, width), F32), sem, sem, pltpu.VMEM((n, 2, width), F32), sem, sem]
+                pltpu.VMEM((4, width), F32), pltpu.VMEM((2, width), F32), pltpu.VMEM((n // 2, 2, width), F32), pltpu.VMEM((2, width), F32),
+                pltpu.VMEM((2, width), F32), pltpu.SemaphoreType.DMA((2, 2)), pltpu.SemaphoreType.DMA((n // 2,)), pltpu.SemaphoreType.DMA((n // 2,)),
+                pltpu.VMEM((n, 2, width), F32), sem, sem,
+                pltpu.VMEM((width, units), F32), pltpu.VMEM((units, width), F32), pltpu.VMEM((dim, width), F32), pltpu.VMEM((1, 3 * dim), F32),
+                pltpu.SemaphoreType.DMA((3,))]
     outs = [((width, units), F32), ((units, width), F32), ((1, units), F32), ((dim, width), F32), ((rows, width), BF16),
-            (w_t.shape, F32), ((1, 3 * dim), F32), ((6, width), F32)]
+            (w_t.shape, F32), ((3, 1, dim), F32), ((6, width), F32)]
     return pl.pallas_call(
         functools.partial(layer_kernel, n, len(hbm)),
         in_specs=[pl.BlockSpec(memory_space=pl.ANY)] * len(hbm) + [vm] * 4,
-        out_specs=[vm] * len(outs),
+        out_specs=[pl.BlockSpec(memory_space=pl.ANY) if i in (0, 1, 3) else vm for i in range(len(outs))],
         out_shape=[jax.ShapeDtypeStruct(*o) for o in outs],
         scratch_shapes=scratch,
         compiler_params=pltpu.CompilerParams(collective_id=1, has_side_effects=True, vmem_limit_bytes=67043328),
@@ -565,24 +636,37 @@
     )(*hbm, gain2, bias2, gain1, bias1)
 
 
-def deliver_kernel(count, *refs):
+def deliver_kernel(pieces, *refs):
+    count = (len(refs) - 2) // 3
+    src, dst, buf, (in_sem, out_sem) = refs[:count], refs[count:2 * count], refs[2 * count:3 * count], refs[3 * count:]
+    into, out = [], []
     for i in range(count):
-        refs[count + i][...] = refs[i][...]
-
-
-def deliver(big, small, steps=4):
-    cut = [pl.BlockSpec((a.shape[0] // steps, a.shape[1]), lambda i: (i, 0)) for a in big]
-    whole = [pl.BlockSpec(a.shape, lambda i: (0, 0)) for a in small]
-    args = list(big) + list(small)
+        size = src[i].shape[0] // pieces[i]
+        for j in range(pieces[i]):
+            rows = slice(j * size, (j + 1) * size)
+            into.append(pltpu.make_async_copy(src[i].at[rows], buf[i].at[rows], in_sem.at[len(into)]))
+            out.append(pltpu.make_async_copy(buf[i].at[rows], dst[i].at[rows], out_sem.at[len(out)]))
+    for c in into:
+        c.start()
+    for a, b in zip(into, out):
+        a.wait()
+        b.start()
+    for b in out:
+        b.wait()
+
+
+def deliver(arrays):
+    pieces = [2 if a.ndim == 2 and a.shape[0] % 32 == 0 else 1 for a in arrays]
+    sems = pltpu.SemaphoreType.DMA((sum(pieces),))
     return pl.pallas_call(
-        functools.partial(deliver_kernel, len(args)),
-        grid=(steps,),
-        in_specs=cut + whole,
-        out_specs=cut + whole,
-        out_shape=[jax.ShapeDtypeStruct(a.shape, a.dtype) for a in args],
-        compiler_params=pltpu.CompilerParams(dimension_semantics=("arbitrary",), vmem_limit_bytes=67043328),
+        functools.partial(deliver_kernel, pieces),
+        in_specs=[pl.BlockSpec(memory_space=pl.ANY)] * len(arrays),
+        out_specs=[pl.BlockSpec(memory_space=pl.ANY)] * len(arrays),
+        out_shape=[jax.ShapeDtypeStruct(a.shape, a.dtype) for a in arrays],
+        scratch_shapes=[pltpu.VMEM(a.shape, a.dtype) for a in arrays] + [sems, sems],
+        compiler_params=pltpu.CompilerParams(vmem_limit_bytes=67043328),
         name="deliver",
-    )(*args)
+    )(*arrays)
 
 
 def solution(mesh):
@@ -595,9 +679,9 @@
         dw1, dw2, db1, dwo, dx, dw_t, db, vecs = layer_stage(
             n, d_out[0], x_mid[0], z_saved[0], w_fc1, w_fc2, q_t, k_t, v_t, w_proj[0], x_in[0], w_qkv_t,
             row(ln2_gain), row(ln2_bias), row(ln1_gain), row(ln1_bias))
-        dx, dw_t, dwo, dw1, dw2, db1, db, vecs = deliver((dx, dw_t, dwo, dw1, dw2), (db1, db, vecs))
+        dw1, dw2, dwo, dw_t, dx, db1, db, vecs = deliver((dw1, dw2, dwo, dw_t, dx, db1, db, vecs))
         grad_wqkv = jnp.transpose(dw_t.reshape(3, dim, -1), (0, 2, 1))[:, :, None, :]
-        return dx[None], grad_wqkv, db.reshape(3, 1, dim), dwo[None], dw1, db1[0], dw2, vecs
+        return dx[None], grad_wqkv, db, dwo[None], dw1, db1[0], dw2, vecs
 
     tok_spec = P('dp', 'tp', None)
     head_spec = P('dp', None, 'tp', None)

time: 294 us -> 285 us (0.969)
  Pallas kernels: 290 us -> 283 us
    pallas_call x1, Pallas kernels: 286 us -> 280 us  [layer_stage(): pl.pallas_call(functools.partial(layer_kernel, n, len(hbm)), in_specs=[pl...]
where the time goes in v5:
time: 285 us; the launch traced here: 284 us
  Pallas kernels  283 us (99%)
    pallas_call x1, Pallas kernels, layer_stage(): pl.pallas_call(functools.partial(layer_kernel, n, len(hbm)), in_specs=[pl...  280 us

profile of v5, /device:TPU:21, one launch (start us, length us, event | category | flops | bytes accessed | tf_op | source)
XLA Modules:
  0.0 284.3 jit_solution(6405526772079725835)
XLA Ops:
  0.6 280.4 %layer_stage.1 = (f32[1024,256]{1,0:T(8,128)}, f32[256,1024]{1,0:T(8,128)}, f32[1,256]{1,0:T(1,128)}, f32[64,1024]{1,0:T(8,128)}, bf16[256,1024]{1,0:T(8,128)(2,...) custom-call(bf16[256,1024]{1,0:T(8,128)(2,1)} %bitcast.32, bf16[256,1024]{1,0:T(8,128)(2,1)} %bitcast.33, ...), custom_call_target="tpu_custom_call" | custom-call | tf_op jit(solution)/shard_map/layer_stage/pallas_call | solution.py:628
  281.0 3.1 %deliver.1 = (f32[1024,256]{1,0:T(8,128)}, f32[256,1024]{1,0:T(8,128)}, f32[64,1024]{1,0:T(8,128)}, f32[192,1024]{1,0:T(8,128)}, bf16[256,1024]{1,0:T(8,128)(2,1...) custom-call(f32[1024,256]{1,0:T(8,128)} %get-tuple-element.24.refs_0_, ...), custom_call_target="tpu_custom_call" | custom-call | tf_op jit(solution)/shard_map/deliver/pallas_call | solution.py:661

commit v6 on v5

--- a/solution.py
+++ b/solution.py
@@ -127,7 +127,7 @@
 
 
 MESH = pl.DeviceIdType.MESH
-SUBS = 2
+SUBS = 4
 
 
 def dot_nt(a, b):
@@ -418,7 +418,7 @@
     half, chips = place.half, place.chips
     seq = kT.shape[1]
     blk = seq // chips
-    gy, gh, gm, g1 = (Gather(subs, place, buf, *gathers[4 * i:4 * i + 4]) for i, (subs, buf) in enumerate(((1, gy_buf), (1, gh_buf), (SUBS, gy_buf), (SUBS, gh_buf))))
+    gy, gh, gm, g1 = (Gather(subs, place, buf, *gathers[4 * i:4 * i + 4]) for i, (subs, buf) in enumerate(((1, gy_buf), (1, gh_buf), (2, gy_buf), (2, gh_buf))))
     rs2, rs1 = (Scatter(subs, place, *rs_bufs, *scatters[4 * i:4 * i + 4]) for i, subs in enumerate((1, SUBS)))
     first_rows, last_rows = PairSpread(place, early, *e_refs), Spread(place, late_part, l_buf, l_send, l_recv)
     mine = pl.ds(pl.multiple_of(place.me * rows_here, rows_here), rows_here)
@@ -581,11 +581,16 @@
         return 0
     lax.fori_loop(1, chips, qkv_step, 0)
 
+    inv_stds = []
+    for d in (0, 1):
+        x_hat, inv_std, _ = layer_norm_fwd(x_in[d * half:(d + 1) * half, :], gain1[...], bias1[...])
+        rs1.keep[d] = x_hat
+        inv_stds.append(inv_std)
     vec = jnp.zeros((2, width), F32)
     for d in (0, 1):
         rows = slice(d * half, (d + 1) * half)
-        x_hat, inv_std, _ = layer_norm_fwd(x_in[rows, :], gain1[...], bias1[...])
         grad = rs1.final(d, rs1.own)
+        x_hat, inv_std = rs1.keep[d], inv_stds[d]
         dx_out[rows, :] = (gy_buf[way[d], :].astype(F32) + layer_norm_bwd(grad, x_hat, inv_std, gain1[...])).astype(BF16)
         vec += jnp.concatenate([jnp.sum(grad * x_hat, axis=0, keepdims=True), jnp.sum(grad, axis=0, keepdims=True)], axis=0)
     late_part[...] = vec

time: 285 us -> 289 us (1.014)
  Pallas kernels: 283 us -> 287 us
    pallas_call x1, Pallas kernels: 280 us -> 284 us  [layer_stage(): pl.pallas_call(functools.partial(layer_kernel, n, len(hbm)), in_specs=[pl...]
where the time goes in v6:
time: 289 us; the launch traced here: 288 us
  Pallas kernels  287 us (99%)
    pallas_call x1, Pallas kernels, layer_stage(): pl.pallas_call(functools.partial(layer_kernel, n, len(hbm)), in_specs=[pl...  284 us

profile of v6, /device:TPU:21, one launch (start us, length us, event | category | flops | bytes accessed | tf_op | source)
XLA Modules:
  0.0 288.1 jit_solution(16055165245045932601)
XLA Ops:
  0.6 284.1 %layer_stage.1 = (f32[1024,256]{1,0:T(8,128)}, f32[256,1024]{1,0:T(8,128)}, f32[1,256]{1,0:T(1,128)}, f32[64,1024]{1,0:T(8,128)}, bf16[256,1024]{1,0:T(8,128)(2,...) custom-call(bf16[256,1024]{1,0:T(8,128)(2,1)} %bitcast.32, bf16[256,1024]{1,0:T(8,128)(2,1)} %bitcast.33, ...), custom_call_target="tpu_custom_call" | custom-call | tf_op jit(solution)/shard_map/layer_stage/pallas_call | solution.py:633
  284.8 3.1 %deliver.1 = (f32[1024,256]{1,0:T(8,128)}, f32[256,1024]{1,0:T(8,128)}, f32[64,1024]{1,0:T(8,128)}, f32[192,1024]{1,0:T(8,128)}, bf16[256,1024]{1,0:T(8,128)(2,1...) custom-call(f32[1024,256]{1,0:T(8,128)} %get-tuple-element.24.refs_0_, ...), custom_call_target="tpu_custom_call" | custom-call | tf_op jit(solution)/shard_map/deliver/pallas_call | solution.py:666
